TPU v7x, 128 devices: a whole 4x4x4 slice. The times are simulated.
128 devices in a mesh: subj: 4 (over y_lo, core), vox: 32 (over z, x, y_hi).
Axes of the slice: x: 4, y: 4 (y_hi: 2, y_lo: 2; y = y_hi * 2 + y_lo), z: 4, core: 2. Of those that a mesh axis runs over, the one named last changes fastest.
Arguments:
- series: bfloat16 [16, 256, 16384], P('subj', None, 'vox'), may hold values from -6 to 6
- offsets: int32 [16, 12], replicated, may hold values from 0 to 240
- selected: int32 [64], replicated, may hold values from 0 to 16383, as said below
Outputs:
- kernel: float32 [64, 192, 192], P('vox', 'subj')
Inputs may be any that keep to these rules, and one draw needn't show every extreme that they name: `offsets`: each epoch lies inside its subject's run; epochs may intersect. `selected`: the ids are distinct.
All inputs are finite; a program needn't handle non-finite values.
Results may differ from a plain program's by a relative error of at most 0.00035.
Values may be sent and summed in bfloat16 or wider, within the bound.
A program may use at most 128 MiB of HBM per device.

v0:
```python
import functools

import jax
import jax.numpy as jnp
from jax import lax
from jax.experimental import pallas as pl
from jax.experimental.pallas import tpu as pltpu
from jax.sharding import PartitionSpec as P

MESH = pl.DeviceIdType.MESH
F32, BF16, I32 = jnp.float32, jnp.bfloat16, jnp.int32
HIGH = lax.Precision.HIGHEST

SUBJ, SHARDS = 4, 32
TR, EP, RUN = 16, 12, 256
LOCAL = 4
QUADS = 3
SEL, OWN = 64, 16
VOX = 512
ROWS = SUBJ * EP * LOCAL
NT = (((1,), (1,)), ((), ()))
series_floor = 1.0
spread_floor = 0.05
shrink_factor = 0.9


def copy_to(src, dst, send_sem, recv_sem, subj, vox):
    return pltpu.make_async_remote_copy(
        src_ref=src,
        dst_ref=dst,
        send_sem=send_sem,
        recv_sem=recv_sem,
        device_id={"subj": subj, "vox": vox},
        device_id_type=MESH,
    )


def await_bytes(ref, sem):
    pltpu.make_async_copy(ref, ref, sem).wait()


def fold(x):
    return x + pltpu.roll(x, 4, 0)


def main_kernel(
    series_hbm,
    offsets,
    selected,
    out_ref,
    series,
    choose,
    epochs,
    scale,
    slab_out,
    slab_in,
    slab_sum,
    slab,
    raw,
    lhs_hi,
    lhs_lo,
    std_hi,
    std_lo,
    corr,
    score,
    gram,
    parts,
    total,
    final,
    load_sem,
    slab_send,
    slab_recv,
    share_send,
    share_recv,
    near_send,
    near_recv,
    far_send,
    far_recv,
    relay_send,
    relay_recv,
    part_send,
    part_recv,
    final_send,
    final_recv,
):
    j = lax.axis_index("subj")
    v = lax.axis_index("vox")
    near, far = j ^ 1, j ^ 2

    load = pltpu.make_async_copy(series_hbm, series, load_sem)
    load.start()

    barrier = pltpu.get_barrier_semaphore()

    def greet(step, carry):
        index = lax.rem(j * SHARDS + v + step, SUBJ * SHARDS)
        pl.semaphore_signal(
            barrier,
            inc=1,
            device_id={"subj": index // SHARDS, "vox": lax.rem(index, SHARDS)},
            device_id_type=MESH,
        )
        return carry

    lax.fori_loop(1, SUBJ * SHARDS, greet, 0)

    row16 = lax.broadcasted_iota(I32, (16, 128), 0)
    scan = lax.broadcasted_iota(I32, (16, LOCAL * RUN), 1)

    for q in range(QUADS):
        start = jnp.zeros((16, 128), I32)
        for r in range(16):
            first = offsets[j * LOCAL + r % 4, q * 4 + r // 4] + (r % 4) * RUN
            start = jnp.where(row16 == r, first, start)
        ahead = scan - jnp.concatenate([start] * (LOCAL * RUN // 128), axis=1)
        for t in range(TR):
            choose[pl.ds(q * 256 + t * 16, 16), :] = jnp.where(ahead == t, 1.0, 0.0).astype(BF16)

    id_rows = []
    row8 = lax.broadcasted_iota(I32, (8, 128), 0)
    for block in range(SEL // 8):
        ids = jnp.zeros((8, 128), I32)
        for r in range(8):
            place = block * 8 + r
            ids = jnp.where(row8 == r, selected[4 * (place % OWN) + place // OWN], ids)
        id_rows.append(ids)
    ids = jnp.concatenate(id_rows, axis=0)
    columns = lax.broadcasted_iota(I32, (SEL, VOX), 1) + v * VOX
    picker = jnp.where(columns == jnp.concatenate([ids] * (VOX // 128), axis=1), 1.0, 0.0).astype(BF16)

    load.wait()
    runs = series[...].reshape(LOCAL * RUN, VOX)
    for q in range(QUADS):
        chosen = jnp.dot(choose[pl.ds(q * 256, 256), :], runs, preferred_element_type=F32).astype(BF16)
        epochs[0, q] = chosen
        slab_out[:, 0, pl.ds(q * 256, 256)] = lax.dot_general(picker, chosen, NT, preferred_element_type=F32)

    pl.semaphore_wait(barrier, SUBJ * SHARDS - 1)

    def send_slab(step, carry):
        piece = lax.rem(v + step, SHARDS)
        to_j, to_v = piece // 8, j * 8 + lax.rem(piece, 8)

        @pl.when(jnp.logical_or(to_j != j, to_v != v))
        def _():
            copy_to(slab_out.at[pl.ds(piece * 2, 2)], slab_in.at[v], slab_send, slab_recv, to_j, to_v).start()

        return carry

    lax.fori_loop(0, SHARDS, send_slab, 0)

    for q in range(QUADS):
        copy_to(epochs.at[0, q], epochs.at[1, q], near_send.at[q], near_recv.at[q], near, v).start()
        copy_to(epochs.at[0, q], epochs.at[2, q], far_send.at[q], far_recv.at[q], far, v).start()

    def scales(r, carry):
        for q in range(QUADS):
            y = epochs[r, q].astype(F32).reshape(TR, 16, VOX)
            centred = y - (jnp.sum(y, axis=0) * (1.0 / TR))[None]
            scale[r, q] = lax.rsqrt(jnp.sum(centred * centred, axis=0) + series_floor)
        return carry

    lax.fori_loop(0, 1, scales, 0)

    own_group = v // 8 == j

    @pl.when(own_group)
    def _():
        slab_in[v] = slab_out[pl.ds((j * 8 + lax.rem(v, 8)) * 2, 2)]
        await_bytes(slab_in.at[pl.ds(0, SHARDS - 1)], slab_recv)
        await_bytes(slab_in.at[pl.ds(0, SHARDS - 1)], slab_send)

    @pl.when(jnp.logical_not(own_group))
    def _():
        await_bytes(slab_in, slab_recv)
        await_bytes(slab_in, slab_send)

    slab_sum[...] = jnp.sum(slab_in[...], axis=0)

    def share_slab(step, carry):
        to_v = lax.rem(v + step, SHARDS)
        copy_to(slab_sum, slab.at[v], share_send, share_recv, j, to_v).start()
        return carry

    lax.fori_loop(1, SHARDS, share_slab, 0)
    slab[v] = slab_sum[...]

    for q in range(QUADS):
        copy_to(epochs.at[0, q], epochs.at[1, q], near_send.at[q], near_recv.at[q], near, v).wait_recv()
    lax.fori_loop(1, 2, scales, 0)

    def relay(q):
        copy_to(epochs.at[0, q], epochs.at[2, q], far_send.at[q], far_recv.at[q], far, v).wait_recv()
        copy_to(epochs.at[2, q], epochs.at[3, q], relay_send.at[q], relay_recv.at[q], near, v).start()

    relay(0)
    await_bytes(slab.at[pl.ds(0, SHARDS - 1)], share_recv)
    await_bytes(slab.at[pl.ds(0, SHARDS - 1)], share_send)

    for r in range(SUBJ):
        group = (j ^ r) if r else j
        for kk in range(8):
            for i in range(2):
                for q in range(QUADS):
                    raw[r * QUADS + q, pl.ds(kk * 2 + i, 1), :] = slab[group * 8 + kk, i, :, pl.ds(q * 256, 256)]
    x = raw[...].reshape(SUBJ * QUADS * OWN, 256)
    same = jnp.where(
        lax.rem(lax.broadcasted_iota(I32, (256, 256), 0), 16) == lax.rem(lax.broadcasted_iota(I32, (256, 256), 1), 16),
        1.0,
        0.0,
    )
    centred = x - jnp.dot(x, same, precision=HIGH, preferred_element_type=F32) * (1.0 / TR)
    spread = jnp.dot(centred * centred, same, precision=HIGH, preferred_element_type=F32)
    x_std = centred * lax.rsqrt(spread + series_floor) * shrink_factor
    x_hi = x_std.astype(BF16).astype(F32)
    std_hi[...] = x_hi.reshape(SUBJ * QUADS, OWN, 256)
    std_lo[...] = (x_std - x_hi).reshape(SUBJ * QUADS, OWN, 256)

    own_row = lax.rem(lax.broadcasted_iota(I32, (16, 256), 1), 16) == lax.broadcasted_iota(I32, (16, 256), 0)

    def group_scores(r, carry):
        def correlate(q, carry):
            for k in range(OWN):
                for std, lhs in ((std_hi, lhs_hi), (std_lo, lhs_lo)):
                    line = jnp.broadcast_to(std[r * QUADS + q, pl.ds(k, 1), :], (16, 256))
                    lhs[pl.ds(k * 16, 16), :] = jnp.where(own_row, line, 0.0).astype(BF16)
            y = epochs[r, q]
            corr[q] = jnp.dot(lhs_hi[...], y, preferred_element_type=F32) + jnp.dot(
                lhs_lo[...], y, preferred_element_type=F32
            )
            return carry

        lax.fori_loop(0, QUADS, correlate, 0)

        def standard(k, carry):
            rows = pl.ds(pl.multiple_of(k * 16, 16), 16)
            twice = []
            for q in range(QUADS):
                shrunk = corr[q, rows, :] * scale[r, q]
                twice.append(jnp.log(1.0 + shrunk) - jnp.log(1.0 - shrunk))
            halves = [f[h * 8 : h * 8 + 8] for f in twice for h in range(2)]
            mean = fold(functools.reduce(jnp.add, halves)) * (1.0 / EP)
            halves = [f - mean for f in halves]
            spread = fold(functools.reduce(jnp.add, [f * f for f in halves])) * (1.0 / EP)
            gain = lax.rsqrt(spread + 4.0 * spread_floor)
            for q in range(QUADS):
                both = jnp.concatenate([halves[2 * q] * gain, halves[2 * q + 1] * gain], axis=0).astype(BF16)
                at = pl.multiple_of(r * 48 + q * 16, 16)
                score[k, pl.ds(at, 16), :] = both

                @pl.when(at < 64)
                def _():
                    score[k, pl.ds(pl.multiple_of(ROWS + lax.rem(at, 64), 16), 16), :] = both

            return carry

        lax.fori_loop(0, OWN, standard, 0)
        return carry

    lax.fori_loop(0, 1, group_scores, 0)
    relay(1)
    lax.fori_loop(1, 2, group_scores, 0)
    relay(2)
    lax.fori_loop(2, 3, scales, 0)
    lax.fori_loop(2, 3, group_scores, 0)
    for q in range(QUADS):
        copy_to(epochs.at[2, q], epochs.at[3, q], relay_send.at[q], relay_recv.at[q], near, v).wait_recv()
    lax.fori_loop(3, 4, scales, 0)
    lax.fori_loop(3, 4, group_scores, 0)

    def kernels(step, carry):
        m = lax.rem(v // 2 + step, OWN)
        for i in range(3):
            gram[m, pl.ds(i * 64, 64), :] = lax.dot_general(
                score[m, pl.ds(i * 64, 64), :], score[m, pl.ds(i * 64, 128), :], NT, preferred_element_type=F32
            )
        for h in range(2):
            to_v = m * 2 + h

            @pl.when(to_v != v)
            def _():
                copy_to(gram.at[m, pl.ds(h * 96, 96)], parts.at[v], part_send, part_recv, j, to_v).start()

        return carry

    lax.fori_loop(0, OWN, kernels, 0)

    parts[v] = gram[v // 2, pl.ds(pl.multiple_of(lax.rem(v, 2) * 96, 8), 96), :]
    await_bytes(parts.at[pl.ds(0, SHARDS - 1)], part_recv)

    def add(i, acc):
        return acc + parts[i]

    total[...] = lax.fori_loop(0, SHARDS, add, jnp.zeros((96, 128), F32)) * (1.0 / (VOX * SHARDS))

    half = lax.rem(v, 2)
    owner_v = v - half + j // 2
    place = lax.rem(j, 2)
    for s in range(SUBJ):

        @pl.when(jnp.logical_or(j != s, owner_v != v))
        def _():
            copy_to(total, final.at[place * 2 + half], final_send, final_recv, s, owner_v).start()

    @pl.when(owner_v == v)
    def _():
        final[place * 2 + half] = total[...]
        await_bytes(final.at[pl.ds(0, SUBJ - 1)], final_recv)
        await_bytes(final.at[pl.ds(0, SUBJ - 1)], final_send)

    @pl.when(owner_v != v)
    def _():
        await_bytes(final, final_recv)
        await_bytes(final, final_send)

    for i in range(2):
        for h in range(2):
            out_ref[i, pl.ds(h * 96, 96), :] = final[i * 2 + h]

    await_bytes(parts.at[pl.ds(0, SHARDS - 1)], part_send)
    for q in range(QUADS):
        copy_to(epochs.at[0, q], epochs.at[1, q], near_send.at[q], near_recv.at[q], near, v).wait_send()
        copy_to(epochs.at[0, q], epochs.at[2, q], far_send.at[q], far_recv.at[q], far, v).wait_send()
        copy_to(epochs.at[2, q], epochs.at[3, q], relay_send.at[q], relay_recv.at[q], near, v).wait_send()


def line_of(group, epoch, subject):
    return group * (EP * LOCAL) + epoch * LOCAL + subject


def place_kernel(cyclic_ref, out_ref):
    j = lax.axis_index("subj")
    v = lax.axis_index("vox")

    def column_line(b, taker):
        s = b // EP
        return line_of((s // LOCAL) ^ taker, lax.rem(b, EP), lax.rem(s, LOCAL))

    for i in range(2):
        taker = lax.rem(v, 2) * 2 + i
        out = jnp.zeros((EP * LOCAL, ROWS), F32)
        for block in range(3):
            part = cyclic_ref[i, pl.ds(block * 64, 64), :]
            c = lax.broadcasted_iota(I32, (128, ROWS), 0)
            to = column_line(lax.broadcasted_iota(I32, (128, ROWS), 1), taker)
            weight = jnp.where(c < 64, 0.5, 1.0)
            wide = jnp.where(lax.rem(block * 64 + c, ROWS) == to, weight, 0.0)
            c = lax.broadcasted_iota(I32, (64, ROWS), 0)
            to = column_line(lax.broadcasted_iota(I32, (64, ROWS), 1), taker)
            tall = jnp.where(block * 64 + c == to, 1.0, 0.0)
            p = lax.broadcasted_iota(I32, (EP * LOCAL, 64), 0)
            line = line_of(j ^ taker, lax.rem(p, EP), p // EP)
            rows = jnp.where(block * 64 + lax.broadcasted_iota(I32, (EP * LOCAL, 64), 1) == line, 1.0, 0.0)
            p = lax.broadcasted_iota(I32, (EP * LOCAL, 128), 0)
            line = line_of(j ^ taker, lax.rem(p, EP), p // EP)
            c = lax.broadcasted_iota(I32, (EP * LOCAL, 128), 1)
            weight = jnp.where(c < 64, 0.5, 1.0)
            turned = jnp.where(lax.rem(block * 64 + c, ROWS) == line, weight, 0.0)
            dot = functools.partial(jnp.dot, precision=HIGH, preferred_element_type=F32)
            out += dot(dot(rows, part), wide)
            out += dot(lax.dot_general(turned, part, NT, precision=HIGH, preferred_element_type=F32), tall)
        out_ref[i] = out


def body(series, offsets, selected):
    vmem = pltpu.VMEM
    dma = pltpu.SemaphoreType.DMA
    cyclic = pl.pallas_call(
        main_kernel,
        out_shape=jax.ShapeDtypeStruct((2, ROWS, 128), F32),
        in_specs=[
            pl.BlockSpec(memory_space=pl.ANY),
            pl.BlockSpec(memory_space=pltpu.SMEM),
            pl.BlockSpec(memory_space=pltpu.SMEM),
        ],
        out_specs=pl.BlockSpec(memory_space=pltpu.VMEM),
        scratch_shapes=[
            vmem((LOCAL, RUN, VOX), BF16),
            vmem((QUADS * 256, LOCAL * RUN), BF16),
            vmem((SUBJ, QUADS, 256, VOX), BF16),
            vmem((SUBJ, QUADS, 16, VOX), F32),
            vmem((SEL, 1, QUADS * 256), F32),
            vmem((SHARDS, 2, 1, QUADS * 256), F32),
            vmem((2, 1, QUADS * 256), F32),
            vmem((SHARDS, 2, 1, QUADS * 256), F32),
            vmem((SUBJ * QUADS, OWN, 256), F32),
            vmem((256, 256), BF16),
            vmem((256, 256), BF16),
            vmem((SUBJ * QUADS, OWN, 256), F32),
            vmem((SUBJ * QUADS, OWN, 256), F32),
            vmem((QUADS, 256, VOX), F32),
            vmem((OWN, 256, VOX), BF16),
            vmem((OWN, ROWS, 128), F32),
            vmem((SHARDS, 96, 128), F32),
            vmem((96, 128), F32),
            vmem((SUBJ, 96, 128), F32),
            dma,
            dma,
            dma,
            dma,
            dma,
            dma((QUADS,)),
            dma((QUADS,)),
            dma((QUADS,)),
            dma((QUADS,)),
            dma((QUADS,)),
            dma((QUADS,)),
            dma,
            dma,
            dma,
            dma,
        ],
        compiler_params=pltpu.CompilerParams(collective_id=0, has_side_effects=True),
        cost_estimate=pl.CostEstimate(flops=10**9, bytes_accessed=10**7, transcendentals=10**6),
    )(series, offsets, selected)
    return pl.pallas_call(
        place_kernel,
        out_shape=jax.ShapeDtypeStruct((2, EP * LOCAL, ROWS), F32),
        in_specs=[pl.BlockSpec(memory_space=pltpu.VMEM)],
        out_specs=pl.BlockSpec(memory_space=pltpu.VMEM),
    )(cyclic)


def solution(mesh):
    placed = (P("subj", None, "vox"), P(), P())
    return jax.shard_map(
        body, mesh=mesh, in_specs=placed, out_specs=P("vox", "subj", None), check_vma=False
    )
```

profile of v0, /device:TPU:1, one launch (start us, length us, event | category | flops | bytes accessed | tf_op | source)
XLA Modules:
  0.0 82.8 jit_solution(9908114371833638844)
XLA Ops:
  0.0 79.7 %shard_map.37.cyclic_ref = f32[2,192,128]{2,1,0:T(8,128)} custom-call(bf16[4,256,512]{2,1,0:T(8,128)(2,1)} %series_hbm.1, s32[16,12]{1,0:T(8,128)} %offsets.1, s32[64]{0:T(128)} %selected.1), custom_call_target="tpu_custom_call" | custom-call | flops 1000000000 | bytes 10000000 | tf_op jit(solution)/shard_map/pallas_call | solution.py:368
  79.7 3.1 %shard_map.38 = f32[2,48,192]{2,1,0:T(8,128)} custom-call(f32[2,192,128]{2,1,0:T(8,128)} %shard_map.37.cyclic_ref), custom_call_target="tpu_custom_call" | custom-call | tf_op jit(solution)/shard_map/pallas_call | solution.py:416
where the time goes:
time: 83 us; the launch traced here: 82.8 us
  Pallas kernels  82.8 us (100%)
    pallas_call x1, Pallas kernels, body(): pl.pallas_call(main_kernel, out_shape=jax.ShapeDtypeStruct((2, ROWS, 128)...  79.7 us
    pallas_call x1, Pallas kernels, body(): pl.pallas_call(place_kernel, out_shape=jax.ShapeDtypeStruct((2, EP * LOCA...  3.09 us

commit v1 on v0

--- a/solution.py
+++ b/solution.py
@@ -64,7 +64,11 @@
     corr,
     score,
     gram,
-    parts,
+    z_parts,
+    x_parts,
+    z_sums,
+    x_sums,
+    last_parts,
     total,
     final,
     load_sem,
@@ -79,7 +83,10 @@
     relay_send,
     relay_recv,
     part_send,
-    part_recv,
+    z_recv,
+    x_recv,
+    sum_send,
+    sum_recv,
     final_send,
     final_recv,
 ):
@@ -93,28 +100,32 @@
     barrier = pltpu.get_barrier_semaphore()
 
     def greet(step, carry):
-        index = lax.rem(j * SHARDS + v + step, SUBJ * SHARDS)
-        pl.semaphore_signal(
-            barrier,
-            inc=1,
-            device_id={"subj": index // SHARDS, "vox": lax.rem(index, SHARDS)},
-            device_id_type=MESH,
-        )
+        for other in range(SUBJ):
+            pl.semaphore_signal(
+                barrier,
+                inc=1,
+                device_id={"subj": j ^ other, "vox": (v + step) & (SHARDS - 1)},
+                device_id_type=MESH,
+            )
         return carry
 
-    lax.fori_loop(1, SUBJ * SHARDS, greet, 0)
+    with jax.named_scope("greet"):
+        lax.fori_loop(1, SHARDS, greet, 0, unroll=4)
+        for other in range(1, SUBJ):
+            pl.semaphore_signal(barrier, inc=1, device_id={"subj": j ^ other, "vox": v}, device_id_type=MESH)
 
     row16 = lax.broadcasted_iota(I32, (16, 128), 0)
     scan = lax.broadcasted_iota(I32, (16, LOCAL * RUN), 1)
 
-    for q in range(QUADS):
-        start = jnp.zeros((16, 128), I32)
-        for r in range(16):
-            first = offsets[j * LOCAL + r % 4, q * 4 + r // 4] + (r % 4) * RUN
-            start = jnp.where(row16 == r, first, start)
-        ahead = scan - jnp.concatenate([start] * (LOCAL * RUN // 128), axis=1)
-        for t in range(TR):
-            choose[pl.ds(q * 256 + t * 16, 16), :] = jnp.where(ahead == t, 1.0, 0.0).astype(BF16)
+    with jax.named_scope("choose"):
+        for q in range(QUADS):
+            start = jnp.zeros((16, 128), I32)
+            for r in range(16):
+                first = offsets[j * LOCAL + r % 4, q * 4 + r // 4] + (r % 4) * RUN
+                start = jnp.where(row16 == r, first, start)
+            ahead = scan - jnp.concatenate([start] * (LOCAL * RUN // 128), axis=1)
+            for t in range(TR):
+                choose[pl.ds(q * 256 + t * 16, 16), :] = jnp.where(ahead == t, 1.0, 0.0).astype(BF16)
 
     id_rows = []
     row8 = lax.broadcasted_iota(I32, (8, 128), 0)
@@ -128,14 +139,16 @@
     columns = lax.broadcasted_iota(I32, (SEL, VOX), 1) + v * VOX
     picker = jnp.where(columns == jnp.concatenate([ids] * (VOX // 128), axis=1), 1.0, 0.0).astype(BF16)
 
-    load.wait()
-    runs = series[...].reshape(LOCAL * RUN, VOX)
-    for q in range(QUADS):
-        chosen = jnp.dot(choose[pl.ds(q * 256, 256), :], runs, preferred_element_type=F32).astype(BF16)
-        epochs[0, q] = chosen
-        slab_out[:, 0, pl.ds(q * 256, 256)] = lax.dot_general(picker, chosen, NT, preferred_element_type=F32)
-
-    pl.semaphore_wait(barrier, SUBJ * SHARDS - 1)
+    with jax.named_scope("pick_epochs"):
+        load.wait()
+        runs = series[...].reshape(LOCAL * RUN, VOX)
+        for q in range(QUADS):
+            chosen = jnp.dot(choose[pl.ds(q * 256, 256), :], runs, preferred_element_type=F32).astype(BF16)
+            epochs[0, q] = chosen
+            slab_out[:, 0, pl.ds(q * 256, 256)] = lax.dot_general(picker, chosen, NT, preferred_element_type=F32)
+
+    with jax.named_scope("barrier"):
+        pl.semaphore_wait(barrier, SUBJ * SHARDS - 1)
 
     def send_slab(step, carry):
         piece = lax.rem(v + step, SHARDS)
@@ -147,11 +160,16 @@
 
         return carry
 
-    lax.fori_loop(0, SHARDS, send_slab, 0)
+    with jax.named_scope("send_slab"):
+        lax.fori_loop(0, SHARDS, send_slab, 0)
 
     for q in range(QUADS):
         copy_to(epochs.at[0, q], epochs.at[1, q], near_send.at[q], near_recv.at[q], near, v).start()
+
+    def send_far(q):
         copy_to(epochs.at[0, q], epochs.at[2, q], far_send.at[q], far_recv.at[q], far, v).start()
+
+    send_far(0)
 
     def scales(r, carry):
         for q in range(QUADS):
@@ -160,61 +178,73 @@
             scale[r, q] = lax.rsqrt(jnp.sum(centred * centred, axis=0) + series_floor)
         return carry
 
-    lax.fori_loop(0, 1, scales, 0)
+    with jax.named_scope("scale0"):
+        lax.fori_loop(0, 1, scales, 0)
 
     own_group = v // 8 == j
 
-    @pl.when(own_group)
-    def _():
-        slab_in[v] = slab_out[pl.ds((j * 8 + lax.rem(v, 8)) * 2, 2)]
-        await_bytes(slab_in.at[pl.ds(0, SHARDS - 1)], slab_recv)
-        await_bytes(slab_in.at[pl.ds(0, SHARDS - 1)], slab_send)
-
-    @pl.when(jnp.logical_not(own_group))
-    def _():
-        await_bytes(slab_in, slab_recv)
-        await_bytes(slab_in, slab_send)
-
-    slab_sum[...] = jnp.sum(slab_in[...], axis=0)
+    with jax.named_scope("slab_wait"):
+        @pl.when(own_group)
+        def _():
+            slab_in[v] = slab_out[pl.ds((j * 8 + lax.rem(v, 8)) * 2, 2)]
+            await_bytes(slab_in.at[pl.ds(0, SHARDS - 1)], slab_recv)
+            await_bytes(slab_in.at[pl.ds(0, SHARDS - 1)], slab_send)
+
+        @pl.when(jnp.logical_not(own_group))
+        def _():
+            await_bytes(slab_in, slab_recv)
+            await_bytes(slab_in, slab_send)
+
+    with jax.named_scope("slab_sum"):
+        slab_sum[...] = jnp.sum(slab_in[...], axis=0)
 
     def share_slab(step, carry):
         to_v = lax.rem(v + step, SHARDS)
         copy_to(slab_sum, slab.at[v], share_send, share_recv, j, to_v).start()
         return carry
 
-    lax.fori_loop(1, SHARDS, share_slab, 0)
-    slab[v] = slab_sum[...]
-
-    for q in range(QUADS):
-        copy_to(epochs.at[0, q], epochs.at[1, q], near_send.at[q], near_recv.at[q], near, v).wait_recv()
-    lax.fori_loop(1, 2, scales, 0)
+    with jax.named_scope("share_slab"):
+        lax.fori_loop(1, SHARDS, share_slab, 0)
+        slab[v] = slab_sum[...]
+
+    send_far(1)
+    send_far(2)
+
+    with jax.named_scope("near_wait"):
+        for q in range(QUADS):
+            copy_to(epochs.at[0, q], epochs.at[1, q], near_send.at[q], near_recv.at[q], near, v).wait_recv()
+    with jax.named_scope("scale1"):
+        lax.fori_loop(1, 2, scales, 0)
 
     def relay(q):
         copy_to(epochs.at[0, q], epochs.at[2, q], far_send.at[q], far_recv.at[q], far, v).wait_recv()
         copy_to(epochs.at[2, q], epochs.at[3, q], relay_send.at[q], relay_recv.at[q], near, v).start()
 
-    relay(0)
-    await_bytes(slab.at[pl.ds(0, SHARDS - 1)], share_recv)
-    await_bytes(slab.at[pl.ds(0, SHARDS - 1)], share_send)
-
-    for r in range(SUBJ):
-        group = (j ^ r) if r else j
-        for kk in range(8):
-            for i in range(2):
-                for q in range(QUADS):
-                    raw[r * QUADS + q, pl.ds(kk * 2 + i, 1), :] = slab[group * 8 + kk, i, :, pl.ds(q * 256, 256)]
-    x = raw[...].reshape(SUBJ * QUADS * OWN, 256)
-    same = jnp.where(
-        lax.rem(lax.broadcasted_iota(I32, (256, 256), 0), 16) == lax.rem(lax.broadcasted_iota(I32, (256, 256), 1), 16),
-        1.0,
-        0.0,
-    )
-    centred = x - jnp.dot(x, same, precision=HIGH, preferred_element_type=F32) * (1.0 / TR)
-    spread = jnp.dot(centred * centred, same, precision=HIGH, preferred_element_type=F32)
-    x_std = centred * lax.rsqrt(spread + series_floor) * shrink_factor
-    x_hi = x_std.astype(BF16).astype(F32)
-    std_hi[...] = x_hi.reshape(SUBJ * QUADS, OWN, 256)
-    std_lo[...] = (x_std - x_hi).reshape(SUBJ * QUADS, OWN, 256)
+    with jax.named_scope("relay0"):
+        relay(0)
+    with jax.named_scope("share_wait"):
+        await_bytes(slab.at[pl.ds(0, SHARDS - 1)], share_recv)
+        await_bytes(slab.at[pl.ds(0, SHARDS - 1)], share_send)
+
+    with jax.named_scope("standard_slab"):
+        for r in range(SUBJ):
+            group = (j ^ r) if r else j
+            for kk in range(8):
+                for i in range(2):
+                    for q in range(QUADS):
+                        raw[r * QUADS + q, pl.ds(kk * 2 + i, 1), :] = slab[group * 8 + kk, i, :, pl.ds(q * 256, 256)]
+        x = raw[...].reshape(SUBJ * QUADS * OWN, 256)
+        same = jnp.where(
+            lax.rem(lax.broadcasted_iota(I32, (256, 256), 0), 16) == lax.rem(lax.broadcasted_iota(I32, (256, 256), 1), 16),
+            1.0,
+            0.0,
+        )
+        centred = x - jnp.dot(x, same, precision=HIGH, preferred_element_type=F32) * (1.0 / TR)
+        spread = jnp.dot(centred * centred, same, precision=HIGH, preferred_element_type=F32)
+        x_std = centred * lax.rsqrt(spread + series_floor) * shrink_factor
+        x_hi = x_std.astype(BF16).astype(F32)
+        std_hi[...] = x_hi.reshape(SUBJ * QUADS, OWN, 256)
+        std_lo[...] = (x_std - x_hi).reshape(SUBJ * QUADS, OWN, 256)
 
     own_row = lax.rem(lax.broadcasted_iota(I32, (16, 256), 1), 16) == lax.broadcasted_iota(I32, (16, 256), 0)
 
@@ -257,71 +287,130 @@
         lax.fori_loop(0, OWN, standard, 0)
         return carry
 
-    lax.fori_loop(0, 1, group_scores, 0)
-    relay(1)
-    lax.fori_loop(1, 2, group_scores, 0)
-    relay(2)
-    lax.fori_loop(2, 3, scales, 0)
-    lax.fori_loop(2, 3, group_scores, 0)
-    for q in range(QUADS):
-        copy_to(epochs.at[2, q], epochs.at[3, q], relay_send.at[q], relay_recv.at[q], near, v).wait_recv()
-    lax.fori_loop(3, 4, scales, 0)
-    lax.fori_loop(3, 4, group_scores, 0)
+    with jax.named_scope("scores0"):
+        lax.fori_loop(0, 1, group_scores, 0)
+    with jax.named_scope("relay1"):
+        relay(1)
+    with jax.named_scope("scores1"):
+        lax.fori_loop(1, 2, group_scores, 0)
+    with jax.named_scope("relay2"):
+        relay(2)
+    with jax.named_scope("scores2"):
+        lax.fori_loop(2, 3, scales, 0)
+        lax.fori_loop(2, 3, group_scores, 0)
+    with jax.named_scope("relay_wait"):
+        for q in range(QUADS):
+            copy_to(epochs.at[2, q], epochs.at[3, q], relay_send.at[q], relay_recv.at[q], near, v).wait_recv()
+    with jax.named_scope("scores3"):
+        lax.fori_loop(3, 4, scales, 0)
+        lax.fori_loop(3, 4, group_scores, 0)
+
+    z, x, y = v // 8, lax.rem(v // 2, 4), lax.rem(v, 2)
+
+    def ahead_of(place, step):
+        return (place + step) & 3
+
+    def shard_at(z, x, y):
+        return z * 8 + x * 2 + y
+
+    def rows_of(m, first, last):
+        for top in (first, 64 if first == 0 else 128):
+            bottom = {0: 64, 64: 96, 96: 128, 128: 192}[top]
+            block = top // 64 * 64
+            gram[m, top:bottom, :] = lax.dot_general(
+                score[m, top:bottom, :], score[m, block : block + 128, :], NT, preferred_element_type=F32
+            )
 
     def kernels(step, carry):
-        m = lax.rem(v // 2 + step, OWN)
-        for i in range(3):
-            gram[m, pl.ds(i * 64, 64), :] = lax.dot_general(
-                score[m, pl.ds(i * 64, 64), :], score[m, pl.ds(i * 64, 128), :], NT, preferred_element_type=F32
-            )
-        for h in range(2):
-            to_v = m * 2 + h
-
-            @pl.when(to_v != v)
+        major, minor = step // 4, step & 3
+        m = ahead_of(z, minor) * 4 + ahead_of(x, major)
+        rows_of(m, 0, 96)
+
+        @pl.when(minor == 0)
+        def _():
+            z_parts[major, 0] = gram[m, 0:96, :]
+
+        @pl.when(minor > 0)
+        def _():
+            to_v = shard_at(ahead_of(z, minor), x, y)
+            copy_to(gram.at[m, pl.ds(0, 96)], z_parts.at[major, minor], part_send, z_recv.at[major], j, to_v).start()
+
+        m = ahead_of(z, major) * 4 + ahead_of(x, minor)
+        rows_of(m, 96, 192)
+
+        @pl.when(minor == 0)
+        def _():
+            x_parts[major, 0] = gram[m, 96:192, :]
+
+        @pl.when(minor > 0)
+        def _():
+            to_v = shard_at(z, ahead_of(x, minor), y)
+            copy_to(gram.at[m, pl.ds(96, 96)], x_parts.at[major, minor], part_send, x_recv.at[major], j, to_v).start()
+
+        return carry
+
+    with jax.named_scope("kernels"):
+        lax.fori_loop(0, OWN, kernels, 0)
+
+    for step in range(4):
+        for half_of, parts, recv, sums, to_v in (
+            (0, z_parts, z_recv, z_sums, shard_at(z, ahead_of(x, step), 0)),
+            (1, x_parts, x_recv, x_sums, shard_at(ahead_of(z, step), x, 1)),
+        ):
+            with jax.named_scope("part_wait"):
+                await_bytes(parts.at[step, pl.ds(1, 3)], recv.at[step])
+            sums[step] = (parts[step, 0] + parts[step, 1]) + (parts[step, 2] + parts[step, 3])
+            if step:
+                slot = step * 2 + (y ^ half_of)
+                copy_to(sums.at[step], last_parts.at[slot], sum_send, sum_recv, j, to_v).start()
+            else:
+
+                @pl.when(y == half_of)
+                def _():
+                    last_parts[0] = sums[0]
+
+                @pl.when(y != half_of)
+                def _():
+                    copy_to(sums.at[0], last_parts.at[1], sum_send, sum_recv, j, to_v).start()
+
+    with jax.named_scope("last_wait"):
+        await_bytes(last_parts.at[pl.ds(1, 7)], sum_recv)
+
+    total[...] = jnp.sum(last_parts[...], axis=0) * (1.0 / (VOX * SHARDS))
+
+    with jax.named_scope("final"):
+        half = lax.rem(v, 2)
+        owner_v = v - half + j // 2
+        place = lax.rem(j, 2)
+        for s in range(SUBJ):
+
+            @pl.when(jnp.logical_or(j != s, owner_v != v))
             def _():
-                copy_to(gram.at[m, pl.ds(h * 96, 96)], parts.at[v], part_send, part_recv, j, to_v).start()
-
-        return carry
-
-    lax.fori_loop(0, OWN, kernels, 0)
-
-    parts[v] = gram[v // 2, pl.ds(pl.multiple_of(lax.rem(v, 2) * 96, 8), 96), :]
-    await_bytes(parts.at[pl.ds(0, SHARDS - 1)], part_recv)
-
-    def add(i, acc):
-        return acc + parts[i]
-
-    total[...] = lax.fori_loop(0, SHARDS, add, jnp.zeros((96, 128), F32)) * (1.0 / (VOX * SHARDS))
-
-    half = lax.rem(v, 2)
-    owner_v = v - half + j // 2
-    place = lax.rem(j, 2)
-    for s in range(SUBJ):
-
-        @pl.when(jnp.logical_or(j != s, owner_v != v))
-        def _():
-            copy_to(total, final.at[place * 2 + half], final_send, final_recv, s, owner_v).start()
-
-    @pl.when(owner_v == v)
-    def _():
-        final[place * 2 + half] = total[...]
-        await_bytes(final.at[pl.ds(0, SUBJ - 1)], final_recv)
-        await_bytes(final.at[pl.ds(0, SUBJ - 1)], final_send)
-
-    @pl.when(owner_v != v)
-    def _():
-        await_bytes(final, final_recv)
-        await_bytes(final, final_send)
+                copy_to(total, final.at[place * 2 + half], final_send, final_recv, s, owner_v).start()
+
+        @pl.when(owner_v == v)
+        def _():
+            final[place * 2 + half] = total[...]
+            await_bytes(final.at[pl.ds(0, SUBJ - 1)], final_recv)
+            await_bytes(final.at[pl.ds(0, SUBJ - 1)], final_send)
+
+        @pl.when(owner_v != v)
+        def _():
+            await_bytes(final, final_recv)
+            await_bytes(final, final_send)
 
     for i in range(2):
         for h in range(2):
             out_ref[i, pl.ds(h * 96, 96), :] = final[i * 2 + h]
 
-    await_bytes(parts.at[pl.ds(0, SHARDS - 1)], part_send)
-    for q in range(QUADS):
-        copy_to(epochs.at[0, q], epochs.at[1, q], near_send.at[q], near_recv.at[q], near, v).wait_send()
-        copy_to(epochs.at[0, q], epochs.at[2, q], far_send.at[q], far_recv.at[q], far, v).wait_send()
-        copy_to(epochs.at[2, q], epochs.at[3, q], relay_send.at[q], relay_recv.at[q], near, v).wait_send()
+    with jax.named_scope("drain"):
+        for _ in range(2):
+            await_bytes(z_parts.at[pl.ds(0, 3)], part_send)
+        await_bytes(last_parts.at[pl.ds(1, 7)], sum_send)
+        for q in range(QUADS):
+            copy_to(epochs.at[0, q], epochs.at[1, q], near_send.at[q], near_recv.at[q], near, v).wait_send()
+            copy_to(epochs.at[0, q], epochs.at[2, q], far_send.at[q], far_recv.at[q], far, v).wait_send()
+            copy_to(epochs.at[2, q], epochs.at[3, q], relay_send.at[q], relay_recv.at[q], near, v).wait_send()
 
 
 def line_of(group, epoch, subject):
@@ -391,7 +480,11 @@
             vmem((QUADS, 256, VOX), F32),
             vmem((OWN, 256, VOX), BF16),
             vmem((OWN, ROWS, 128), F32),
-            vmem((SHARDS, 96, 128), F32),
+            vmem((4, 4, 96, 128), F32),
+            vmem((4, 4, 96, 128), F32),
+            vmem((4, 96, 128), F32),
+            vmem((4, 96, 128), F32),
+            vmem((8, 96, 128), F32),
             vmem((96, 128), F32),
             vmem((SUBJ, 96, 128), F32),
             dma,
@@ -405,6 +498,9 @@
             dma((QUADS,)),
             dma((QUADS,)),
             dma((QUADS,)),
+            dma,
+            dma((4,)),
+            dma((4,)),
             dma,
             dma,
             dma,

time: 83 us -> 63.1 us (0.76)
  Pallas kernels: 82.8 us -> 62.8 us
    pallas_call x1, Pallas kernels: 79.7 us -> 59.7 us  [body(): pl.pallas_call(main_kernel, out_shape=jax.ShapeDtypeStruct((2, ROWS, 128)...]
where the time goes in v1:
time: 63.1 us; the launch traced here: 62.8 us
  Pallas kernels  62.8 us (100%)
    pallas_call x1, Pallas kernels, body(): pl.pallas_call(main_kernel, out_shape=jax.ShapeDtypeStruct((2, ROWS, 128)...  59.7 us
    pallas_call x1, Pallas kernels, body(): pl.pallas_call(place_kernel, out_shape=jax.ShapeDtypeStruct((2, EP * LOCA...  3.09 us

profile of v1, /device:TPU:1, one launch (start us, length us, event | category | flops | bytes accessed | tf_op | source)
XLA Modules:
  0.0 62.8 jit_solution(7448392617042563983)
XLA Ops:
  0.0 59.7 %shard_map.37.cyclic_ref = f32[2,192,128]{2,1,0:T(8,128)} custom-call(bf16[4,256,512]{2,1,0:T(8,128)(2,1)} %series_hbm.1, s32[16,12]{1,0:T(8,128)} %offsets.1, s32[64]{0:T(128)} %selected.1), custom_call_target="tpu_custom_call" | custom-call | flops 1000000000 | bytes 10000000 | tf_op jit(solution)/shard_map/pallas_call | solution.py:457
  59.8 3.1 %shard_map.38 = f32[2,48,192]{2,1,0:T(8,128)} custom-call(f32[2,192,128]{2,1,0:T(8,128)} %shard_map.37.cyclic_ref), custom_call_target="tpu_custom_call" | custom-call | tf_op jit(solution)/shard_map/pallas_call | solution.py:512

commit v2 on v1

v2 whole, which is shorter than its diff:
```python
import functools

import jax
import jax.numpy as jnp
from jax import lax
from jax.experimental import pallas as pl
from jax.experimental.pallas import tpu as pltpu
from jax.sharding import PartitionSpec as P

MESH = pl.DeviceIdType.MESH
F32, BF16, I32 = jnp.float32, jnp.bfloat16, jnp.int32
HIGH = lax.Precision.HIGHEST

SUBJ, SHARDS = 4, 32
TR, EP, RUN = 16, 12, 256
LOCAL = 4
QUADS = 3
SEL, OWN = 64, 16
VOX = 512
ROWS = SUBJ * EP * LOCAL
NT = (((1,), (1,)), ((), ()))
series_floor = 1.0
spread_floor = 0.05
shrink_factor = 0.9


def copy_to(src, dst, send_sem, recv_sem, subj, vox):
    return pltpu.make_async_remote_copy(
        src_ref=src,
        dst_ref=dst,
        send_sem=send_sem,
        recv_sem=recv_sem,
        device_id={"subj": subj, "vox": vox},
        device_id_type=MESH,
    )


def await_bytes(ref, sem):
    pltpu.make_async_copy(ref, ref, sem).wait()


def fold(x):
    return x + pltpu.roll(x, 4, 0)


def exact_terms(x):
    first = x.astype(BF16)
    rest = x - first.astype(F32)
    second = rest.astype(BF16)
    return first, second, (rest - second.astype(F32)).astype(BF16)


def line_of(group, epoch, subject):
    return group * (EP * LOCAL) + epoch * LOCAL + subject


def main_kernel(
    series_hbm,
    offsets,
    selected,
    out_ref,
    series,
    choose,
    epochs,
    scale,
    slab_out,
    slab_in,
    slab_sum,
    slab,
    raw,
    lhs_hi,
    lhs_lo,
    std_hi,
    std_lo,
    corr,
    score,
    gram,
    z_parts,
    x_parts,
    y_parts,
    z_sums,
    x_sums,
    y_sums,
    last,
    total,
    final,
    pick_rows,
    pick_turned,
    put_columns,
    load_sem,
    slab_send,
    slab_recv,
    share_send,
    share_recv,
    near_send,
    near_recv,
    far_send,
    far_recv,
    relay_send,
    relay_recv,
    part_send,
    z_recv,
    x_recv,
    y_recv,
    sum_send,
    sum_recv,
    final_send,
    final_recv,
):
    j = lax.axis_index("subj")
    v = lax.axis_index("vox")
    near, far = j ^ 1, j ^ 2
    z, x, y = v // 8, (v // 2) & 3, v & 1

    def ahead_of(place, step):
        return (place + step) & 3

    def shard_at(z, x, y):
        return z * 8 + x * 2 + y

    load = pltpu.make_async_copy(series_hbm, series, load_sem)
    load.start()

    barrier = pltpu.get_barrier_semaphore()

    def greet(step, carry):
        for other in range(SUBJ):
            pl.semaphore_signal(
                barrier,
                inc=1,
                device_id={"subj": j ^ other, "vox": (v + step) & (SHARDS - 1)},
                device_id_type=MESH,
            )
        return carry

    with jax.named_scope("greet"):
        lax.fori_loop(1, SHARDS, greet, 0, unroll=4)
        for other in range(1, SUBJ):
            pl.semaphore_signal(barrier, inc=1, device_id={"subj": j ^ other, "vox": v}, device_id_type=MESH)

    with jax.named_scope("choose"):
        row16 = lax.broadcasted_iota(I32, (16, 128), 0)
        scan = lax.broadcasted_iota(I32, (16, LOCAL * RUN), 1)
        for q in range(QUADS):
            start = jnp.zeros((16, 128), I32)
            for r in range(16):
                first = offsets[j * LOCAL + r % 4, q * 4 + r // 4] + (r % 4) * RUN
                start = jnp.where(row16 == r, first, start)
            ahead = scan - jnp.concatenate([start] * (LOCAL * RUN // 128), axis=1)
            for t in range(TR):
                choose[pl.ds(q * 256 + t * 16, 16), :] = jnp.where(ahead == t, 1.0, 0.0).astype(BF16)

    id_rows = []
    row8 = lax.broadcasted_iota(I32, (8, 128), 0)
    for block in range(SEL // 8):
        ids = jnp.zeros((8, 128), I32)
        for r in range(8):
            place = block * 8 + r
            ids = jnp.where(row8 == r, selected[4 * (place % OWN) + place // OWN], ids)
        id_rows.append(ids)
    ids = jnp.concatenate(id_rows, axis=0)
    columns = lax.broadcasted_iota(I32, (SEL, VOX), 1) + v * VOX
    picker = jnp.where(columns == jnp.concatenate([ids] * (VOX // 128), axis=1), 1.0, 0.0).astype(BF16)

    with jax.named_scope("pick_epochs"):
        load.wait()
        runs = series[...].reshape(LOCAL * RUN, VOX)
        for q in range(QUADS):
            chosen = jnp.dot(choose[pl.ds(q * 256, 256), :], runs, preferred_element_type=F32).astype(BF16)
            epochs[0, q] = chosen
            picked = lax.dot_general(picker, chosen, NT, preferred_element_type=F32)
            slab_out[:, :, pl.ds(q * 256, 256)] = picked.astype(BF16).reshape(SHARDS, 2, 256)

    with jax.named_scope("barrier"):
        pl.semaphore_wait(barrier, SUBJ * SHARDS - 1)

    def send_slab(step, carry):
        piece = (v + step) & (SHARDS - 1)
        to_j, to_v = piece // 8, j * 8 + (piece & 7)

        @pl.when(jnp.logical_or(to_j != j, to_v != v))
        def _():
            copy_to(slab_out.at[piece], slab_in.at[v], slab_send, slab_recv, to_j, to_v).start()

        return carry

    with jax.named_scope("send_slab"):
        lax.fori_loop(0, SHARDS, send_slab, 0)

    def near_copy(q):
        return copy_to(epochs.at[0, q], epochs.at[1, q], near_send.at[q], near_recv.at[q], near, v)

    def half_of(r, h, q):
        return epochs.at[r, q, :, pl.ds(h * 256, 256)]

    def far_copy(h, q):
        at = h * QUADS + q
        return copy_to(half_of(0, h, q), half_of(2, h, q), far_send.at[at], far_recv.at[at], far, v)

    def relay_copy(h, q):
        at = h * QUADS + q
        return copy_to(half_of(2, h, q), half_of(3, h, q), relay_send.at[at], relay_recv.at[at], near, v)

    def relay(h, q):
        with jax.named_scope("relay"):
            far_copy(h, q).wait_recv()
            relay_copy(h, q).start()

    for q in range(QUADS):
        near_copy(q).start()
    far_copy(0, 0).start()
    far_copy(0, 1).start()

    def scales(r, h):
        lanes = pl.ds(h * 256, 256)
        for q in range(QUADS):
            seen = epochs[r, q, :, lanes].astype(F32).reshape(TR, 16, 256)
            centred = seen - (jnp.sum(seen, axis=0) * (1.0 / TR))[None]
            scale[r, q, :, lanes] = lax.rsqrt(jnp.sum(centred * centred, axis=0) + series_floor)

    for h in range(2):
        scales(0, h)

    own_group = v // 8 == j

    with jax.named_scope("slab_wait"):

        @pl.when(own_group)
        def _():
            slab_in[v] = slab_out[j * 8 + (v & 7)]
            await_bytes(slab_in.at[pl.ds(0, SHARDS - 1)], slab_recv)

        @pl.when(jnp.logical_not(own_group))
        def _():
            await_bytes(slab_in, slab_recv)

    with jax.named_scope("slab_sum"):
        slab_sum[...] = jnp.sum(slab_in[...].astype(F32), axis=0).astype(BF16)

    def share_slab(step, carry):
        copy_to(slab_sum, slab.at[v], share_send, share_recv, j, (v + step) & (SHARDS - 1)).start()
        return carry

    with jax.named_scope("share_slab"):
        lax.fori_loop(1, SHARDS, share_slab, 0)
        slab[v] = slab_sum[...]

    far_copy(0, 2).start()
    for q in range(QUADS):
        far_copy(1, q).start()

    with jax.named_scope("places"):
        b = lax.broadcasted_iota(I32, (1, ROWS), 1)
        p = lax.broadcasted_iota(I32, (EP * LOCAL, 1), 0)
        for i in range(2):
            taker = y * 2 + i
            s = b // EP
            to = line_of((s // LOCAL) ^ taker, b - s * EP, s & 3)
            s = p // EP
            line = line_of(j ^ taker, p - s * EP, s)
            c = lax.broadcasted_iota(I32, (ROWS, 1), 0)
            put_columns[i, pl.ds(3 * 128, ROWS), :] = jnp.where(c == to, 1.0, 0.0).astype(BF16)
            for block in range(3):
                c = lax.broadcasted_iota(I32, (128, 1), 0) + block * 64
                c = jnp.where(c < ROWS, c, c - ROWS)
                weight = jnp.where(lax.broadcasted_iota(I32, (128, ROWS), 0) < 64, 0.5, 1.0)
                put_columns[i, pl.ds(block * 128, 128), :] = jnp.where(c == to, weight, 0.0).astype(BF16)
                c = lax.broadcasted_iota(I32, (1, 128), 1) + block * 64
                c = jnp.where(c < ROWS, c, c - ROWS)
                weight = jnp.where(lax.broadcasted_iota(I32, (EP * LOCAL, 128), 1) < 64, 0.5, 1.0)
                pick_turned[i, block] = jnp.where(c == line, weight, 0.0).astype(BF16)
                c = lax.broadcasted_iota(I32, (1, 64), 1) + block * 64
                pick_rows[i, block] = jnp.where(c == line, 1.0, 0.0).astype(BF16)

    with jax.named_scope("near_wait"):
        for q in range(QUADS):
            near_copy(q).wait_recv()
    for h in range(2):
        scales(1, h)

    relay(0, 0)
    relay(0, 1)
    with jax.named_scope("share_wait"):
        await_bytes(slab.at[pl.ds(0, SHARDS - 1)], share_recv)

    with jax.named_scope("standard_slab"):
        for r in range(SUBJ):
            group = (j ^ r) if r else j
            for kk in range(8):
                for q in range(QUADS):
                    raw[r * QUADS + q, pl.ds(kk * 2, 2), :] = slab[group * 8 + kk, :, pl.ds(q * 256, 256)].astype(F32)
        seen = raw[...].reshape(SUBJ * QUADS * OWN, 256)
        same = jnp.where(
            (lax.broadcasted_iota(I32, (256, 256), 0) & 15) == (lax.broadcasted_iota(I32, (256, 256), 1) & 15), 1.0, 0.0
        )
        centred = seen - jnp.dot(seen, same, precision=HIGH, preferred_element_type=F32) * (1.0 / TR)
        spread = jnp.dot(centred * centred, same, precision=HIGH, preferred_element_type=F32)
        x_std = centred * lax.rsqrt(spread + series_floor) * shrink_factor
        x_hi = x_std.astype(BF16).astype(F32)
        std_hi[...] = x_hi.reshape(SUBJ * QUADS, OWN, 256)
        std_lo[...] = (x_std - x_hi).reshape(SUBJ * QUADS, OWN, 256)

    own_row = (lax.broadcasted_iota(I32, (16, 256), 1) & 15) == lax.broadcasted_iota(I32, (16, 256), 0)

    def group_scores(r, h):
        lanes = pl.ds(h * 256, 256)

        def correlate(q, carry):
            for k in range(OWN):
                for std, lhs in ((std_hi, lhs_hi), (std_lo, lhs_lo)):
                    line = jnp.broadcast_to(std[r * QUADS + q, pl.ds(k, 1), :], (16, 256))
                    lhs[pl.ds(k * 16, 16), :] = jnp.where(own_row, line, 0.0).astype(BF16)
            seen = epochs[r, q, :, lanes]
            corr[q] = jnp.dot(lhs_hi[...], seen, preferred_element_type=F32) + jnp.dot(
                lhs_lo[...], seen, preferred_element_type=F32
            )
            return carry

        lax.fori_loop(0, QUADS, correlate, 0)

        def standard(k, carry):
            rows = pl.ds(pl.multiple_of(k * 16, 16), 16)
            halves = []
            for q in range(QUADS):
                shrunk = corr[q, rows, :] * scale[r, q, :, lanes]
                twice = jnp.log(1.0 + shrunk) - jnp.log(1.0 - shrunk)
                halves += [twice[0:8], twice[8:16]]
            mean = fold(functools.reduce(jnp.add, halves)) * (1.0 / EP)
            halves = [f - mean for f in halves]
            spread = fold(functools.reduce(jnp.add, [f * f for f in halves])) * (1.0 / EP)
            gain = lax.rsqrt(spread + 4.0 * spread_floor)
            for q in range(QUADS):
                both = jnp.concatenate([halves[2 * q] * gain, halves[2 * q + 1] * gain], axis=0).astype(BF16)
                at = r * 48 + q * 16
                score[k, pl.ds(at, 16), lanes] = both
                if at < 64:
                    score[k, pl.ds(ROWS + at, 16), lanes] = both
            return carry

        lax.fori_loop(0, OWN, standard, 0, unroll=2)

    with jax.named_scope("scores0"):
        group_scores(0, 0)
        group_scores(0, 1)
    relay(0, 2)
    with jax.named_scope("scores1"):
        group_scores(1, 0)
    relay(1, 0)
    with jax.named_scope("scores1"):
        group_scores(1, 1)
    with jax.named_scope("scores2"):
        scales(2, 0)
        group_scores(2, 0)
    relay(1, 1)
    for q in range(QUADS):
        relay_copy(0, q).wait_recv()
    with jax.named_scope("scores3"):
        scales(3, 0)
        group_scores(3, 0)
    relay(1, 2)
    with jax.named_scope("scores4"):
        scales(2, 1)
        group_scores(2, 1)
    for q in range(QUADS):
        relay_copy(1, q).wait_recv()
    with jax.named_scope("scores5"):
        scales(3, 1)
        group_scores(3, 1)

    def block_of(m, block):
        gram[m, pl.ds(block * 64, 64), :] = lax.dot_general(
            score[m, pl.ds(block * 64, 64), :], score[m, pl.ds(block * 64, 128), :], NT, preferred_element_type=F32
        )

    def kernels(step, carry):
        major, minor = step // 4, step & 3
        m = ahead_of(z, minor) * 4 + ahead_of(x, major)
        block_of(m, 0)

        @pl.when(minor == 0)
        def _():
            z_parts[major, 0] = gram[m, 0:64, :]

        @pl.when(minor > 0)
        def _():
            to_v = shard_at(ahead_of(z, minor), x, y)
            copy_to(gram.at[m, pl.ds(0, 64)], z_parts.at[major, minor], part_send, z_recv.at[major], j, to_v).start()

        m = ahead_of(z, major) * 4 + ahead_of(x, minor)
        block_of(m, 1)

        @pl.when(minor == 0)
        def _():
            x_parts[major, 0] = gram[m, 64:128, :]

        @pl.when(minor > 0)
        def _():
            to_v = shard_at(z, ahead_of(x, minor), y)
            copy_to(gram.at[m, pl.ds(64, 64)], x_parts.at[major, minor], part_send, x_recv.at[major], j, to_v).start()

        block_of(m, 2)
        rows = pl.ds(pl.multiple_of(128 + 32 * (y ^ 1), 32), 32)
        copy_to(gram.at[m, rows], y_parts.at[step], part_send, y_recv.at[major], j, v ^ 1).start()
        return carry

    with jax.named_scope("kernels"):
        lax.fori_loop(0, OWN, kernels, 0)

    for major in range(4):
        for block, parts, recv, sums in ((0, z_parts, z_recv, z_sums), (1, x_parts, x_recv, x_sums)):
            with jax.named_scope("part_wait"):
                await_bytes(parts.at[major, pl.ds(1, 3)], recv.at[major])
            sums[major] = (parts[major, 0] + parts[major, 1]) + (parts[major, 2] + parts[major, 3])
            for other in range(2):
                side = y ^ other
                rows = pl.ds(pl.multiple_of(side * 32, 32), 32)
                slot = major * 2 + other
                to_v = shard_at(ahead_of(z, major), x, side) if block else shard_at(z, ahead_of(x, major), side)
                if slot:
                    copy_to(sums.at[major, rows], last.at[block * 8 + slot], sum_send, sum_recv, j, to_v).start()
                else:
                    last[block * 8] = sums[0, rows, :]
        with jax.named_scope("part_wait"):
            await_bytes(y_parts.at[pl.ds(major * 4, 4)], y_recv.at[major])
        for minor in range(4):
            step = major * 4 + minor
            to_z, to_x = ahead_of(z, major), ahead_of(x, minor)
            rows = pl.ds(pl.multiple_of(128 + 32 * y, 32), 32)
            added = y_parts[step] + gram[to_z * 4 + to_x, rows, :]
            if step:
                y_sums[step] = added
                copy_to(y_sums.at[step], last.at[16 + step], sum_send, sum_recv, j, shard_at(to_z, to_x, y)).start()
            else:
                last[16] = added

    with jax.named_scope("last_wait"):
        await_bytes(last.at[pl.ds(0, 29)], sum_recv)

    mean = 1.0 / (VOX * SHARDS)
    total[0:32, :] = jnp.sum(last[0:8], axis=0) * mean
    total[32:64, :] = jnp.sum(last[8:16], axis=0) * mean
    total[64:96, :] = jnp.sum(last[16:32], axis=0) * mean

    owner_v = v - y + j // 2
    place = (j & 1) * 2 + y
    with jax.named_scope("final"):
        for other in range(SUBJ):
            to_j = (j ^ other) if other else j
            if other:
                copy_to(total, final.at[place], final_send, final_recv, to_j, owner_v).start()
            else:

                @pl.when(owner_v != v)
                def _():
                    copy_to(total, final.at[place], final_send, final_recv, j, owner_v).start()

        @pl.when(owner_v == v)
        def _():
            final[place] = total[...]
            await_bytes(final.at[pl.ds(0, SUBJ - 1)], final_recv)

        @pl.when(owner_v != v)
        def _():
            await_bytes(final, final_recv)

    with jax.named_scope("place"):
        for i in range(2):
            taken = []
            for block in range(3):
                rows = pl.ds(block * 32, 32)
                terms = exact_terms(jnp.concatenate([final[2 * i, rows, :], final[2 * i + 1, rows, :]], axis=0))
                wide = [jnp.dot(pick_rows[i, block], t, preferred_element_type=F32) for t in terms]
                tall = [lax.dot_general(pick_turned[i, block], t, NT, preferred_element_type=F32) for t in terms]
                taken.append((wide[0] + wide[1] + wide[2], tall[0] + tall[1] + tall[2]))
            lines = jnp.concatenate([t[0] for t in taken] + [t[1] for t in taken], axis=1)
            terms = [jnp.dot(t, put_columns[i], preferred_element_type=F32) for t in exact_terms(lines)]
            out_ref[i] = terms[0] + terms[1] + terms[2]

    with jax.named_scope("drain"):
        await_bytes(slab_in.at[pl.ds(0, SHARDS - 1)], share_send)

        @pl.when(own_group)
        def _():
            await_bytes(slab_in.at[pl.ds(0, SHARDS - 1)], slab_send)

        @pl.when(jnp.logical_not(own_group))
        def _():
            await_bytes(slab_in, slab_send)

        for _ in range(2):
            await_bytes(z_parts.at[pl.ds(0, 3)], part_send)
        await_bytes(y_parts, part_send)
        await_bytes(last.at[pl.ds(0, 29)], sum_send)

        @pl.when(owner_v == v)
        def _():
            await_bytes(final.at[pl.ds(0, SUBJ - 1)], final_send)

        @pl.when(owner_v != v)
        def _():
            await_bytes(final, final_send)

        for q in range(QUADS):
            near_copy(q).wait_send()
            for h in range(2):
                far_copy(h, q).wait_send()
                relay_copy(h, q).wait_send()


def body(series, offsets, selected):
    vmem = pltpu.VMEM
    dma = pltpu.SemaphoreType.DMA
    return pl.pallas_call(
        main_kernel,
        out_shape=jax.ShapeDtypeStruct((2, EP * LOCAL, ROWS), F32),
        in_specs=[
            pl.BlockSpec(memory_space=pl.ANY),
            pl.BlockSpec(memory_space=pltpu.SMEM),
            pl.BlockSpec(memory_space=pltpu.SMEM),
        ],
        out_specs=pl.BlockSpec(memory_space=pltpu.VMEM),
        scratch_shapes=[
            vmem((LOCAL, RUN, VOX), BF16),
            vmem((QUADS * 256, LOCAL * RUN), BF16),
            vmem((SUBJ, QUADS, 256, VOX), BF16),
            vmem((SUBJ, QUADS, 16, VOX), F32),
            vmem((SHARDS, 2, QUADS * 256), BF16),
            vmem((SHARDS, 2, QUADS * 256), BF16),
            vmem((2, QUADS * 256), BF16),
            vmem((SHARDS, 2, QUADS * 256), BF16),
            vmem((SUBJ * QUADS, OWN, 256), F32),
            vmem((256, 256), BF16),
            vmem((256, 256), BF16),
            vmem((SUBJ * QUADS, OWN, 256), F32),
            vmem((SUBJ * QUADS, OWN, 256), F32),
            vmem((QUADS, 256, 256), F32),
            vmem((OWN, 256, VOX), BF16),
            vmem((OWN, ROWS, 128), F32),
            vmem((4, 4, 64, 128), F32),
            vmem((4, 4, 64, 128), F32),
            vmem((OWN, 32, 128), F32),
            vmem((4, 64, 128), F32),
            vmem((4, 64, 128), F32),
            vmem((OWN, 32, 128), F32),
            vmem((32, 32, 128), F32),
            vmem((96, 128), F32),
            vmem((SUBJ, 96, 128), F32),
            vmem((2, 3, EP * LOCAL, 64), BF16),
            vmem((2, 3, EP * LOCAL, 128), BF16),
            vmem((2, 3 * 128 + ROWS, ROWS), BF16),
            dma,
            dma,
            dma,
            dma,
            dma,
            dma((QUADS,)),
            dma((QUADS,)),
            dma((2 * QUADS,)),
            dma((2 * QUADS,)),
            dma((2 * QUADS,)),
            dma((2 * QUADS,)),
            dma,
            dma((4,)),
            dma((4,)),
            dma((4,)),
            dma,
            dma,
            dma,
            dma,
        ],
        compiler_params=pltpu.CompilerParams(collective_id=0, has_side_effects=True),
    )(series, offsets, selected)


def solution(mesh):
    placed = (P("subj", None, "vox"), P(), P())
    return jax.shard_map(
        body, mesh=mesh, in_specs=placed, out_specs=P("vox", "subj", None), check_vma=False
    )
```

time: 63.1 us -> 60 us (0.951)
  Pallas kernels: 62.8 us -> 58.2 us
  local copies, waits for them, and re-layouts: 0 us -> 1.54 us
    pallas_call x2 -> x1, Pallas kernels: 62.8 us -> 58.2 us  [body(): pl.pallas_call(main_kernel, out_shape=jax.ShapeDtypeStruct((2, EP * LOCAL...]
    unnamed x0 -> x1, local copies, waits for them, and re-layouts: none -> 1.54 us
where the time goes in v2:
time: 60 us; the launch traced here: 59.8 us
  Pallas kernels  58.2 us (97%)
  local copies, waits for them, and re-layouts  1.54 us (3%)
    pallas_call x1, Pallas kernels, body(): pl.pallas_call(main_kernel, out_shape=jax.ShapeDtypeStruct((2, EP * LOCAL...  58.2 us
    unnamed x1, local copies, waits for them, and re-layouts  1.54 us

profile of v2, /device:TPU:1, one launch (start us, length us, event | category | flops | bytes accessed | tf_op | source)
XLA Modules:
  0.0 59.8 jit_solution(4607029624344638913)
XLA Ops:
  0.0 58.2 %shard_map.37 = f32[2,48,192]{2,1,0:T(8,128)} custom-call(bf16[4,256,512]{2,1,0:T(8,128)(2,1)} %series_hbm.1, s32[16,12]{1,0:T(8,128)} %offsets.1, s32[64]{0:T(128)} %selected.1), custom_call_target="tpu_custom_call" | custom-call | tf_op jit(solution)/shard_map/pallas_call | solution.py:513
  58.3 1.5 %copy.5 = f32[2,48,192]{2,1,0:T(8,128)} copy(f32[2,48,192]{2,1,0:T(8,128)} %shard_map.37) | data formatting | bytes 147456

commit v3 on v2

--- a/solution.py
+++ b/solution.py
@@ -56,9 +56,11 @@
 
 def main_kernel(
     series_hbm,
+    offsets_hbm,
+    selected_hbm,
+    out_ref,
     offsets,
     selected,
-    out_ref,
     series,
     choose,
     epochs,
@@ -72,7 +74,8 @@
     lhs_lo,
     std_hi,
     std_lo,
-    corr,
+    corr_even,
+    corr_odd,
     score,
     gram,
     z_parts,
@@ -107,6 +110,7 @@
     final_send,
     final_recv,
 ):
+    corr = (corr_even, corr_odd)
     j = lax.axis_index("subj")
     v = lax.axis_index("vox")
     near, far = j ^ 1, j ^ 2
@@ -118,8 +122,14 @@
     def shard_at(z, x, y):
         return z * 8 + x * 2 + y
 
-    load = pltpu.make_async_copy(series_hbm, series, load_sem)
-    load.start()
+    loads = [
+        pltpu.make_async_copy(source, target, load_sem.at[i])
+        for i, (source, target) in enumerate(
+            ((offsets_hbm, offsets), (selected_hbm, selected), (series_hbm, series))
+        )
+    ]
+    for load in loads:
+        load.start()
 
     barrier = pltpu.get_barrier_semaphore()
 
@@ -137,6 +147,9 @@
         lax.fori_loop(1, SHARDS, greet, 0, unroll=4)
         for other in range(1, SUBJ):
             pl.semaphore_signal(barrier, inc=1, device_id={"subj": j ^ other, "vox": v}, device_id_type=MESH)
+
+    loads[0].wait()
+    loads[1].wait()
 
     with jax.named_scope("choose"):
         row16 = lax.broadcasted_iota(I32, (16, 128), 0)
@@ -163,7 +176,7 @@
     picker = jnp.where(columns == jnp.concatenate([ids] * (VOX // 128), axis=1), 1.0, 0.0).astype(BF16)
 
     with jax.named_scope("pick_epochs"):
-        load.wait()
+        loads[2].wait()
         runs = series[...].reshape(LOCAL * RUN, VOX)
         for q in range(QUADS):
             chosen = jnp.dot(choose[pl.ds(q * 256, 256), :], runs, preferred_element_type=F32).astype(BF16)
@@ -209,7 +222,6 @@
     for q in range(QUADS):
         near_copy(q).start()
     far_copy(0, 0).start()
-    far_copy(0, 1).start()
 
     def scales(r, h):
         lanes = pl.ds(h * 256, 256)
@@ -245,6 +257,7 @@
         lax.fori_loop(1, SHARDS, share_slab, 0)
         slab[v] = slab_sum[...]
 
+    far_copy(0, 1).start()
     far_copy(0, 2).start()
     for q in range(QUADS):
         far_copy(1, q).start()
@@ -292,9 +305,11 @@
         seen = raw[...].reshape(SUBJ * QUADS * OWN, 256)
         same = jnp.where(
             (lax.broadcasted_iota(I32, (256, 256), 0) & 15) == (lax.broadcasted_iota(I32, (256, 256), 1) & 15), 1.0, 0.0
-        )
-        centred = seen - jnp.dot(seen, same, precision=HIGH, preferred_element_type=F32) * (1.0 / TR)
-        spread = jnp.dot(centred * centred, same, precision=HIGH, preferred_element_type=F32)
+        ).astype(BF16)
+        centred = seen - jnp.dot(seen.astype(BF16), same, preferred_element_type=F32) * (1.0 / TR)
+        terms = exact_terms(centred * centred)
+        spread = [jnp.dot(t, same, preferred_element_type=F32) for t in terms]
+        spread = spread[0] + spread[1] + spread[2]
         x_std = centred * lax.rsqrt(spread + series_floor) * shrink_factor
         x_hi = x_std.astype(BF16).astype(F32)
         std_hi[...] = x_hi.reshape(SUBJ * QUADS, OWN, 256)
@@ -302,27 +317,32 @@
 
     own_row = (lax.broadcasted_iota(I32, (16, 256), 1) & 15) == lax.broadcasted_iota(I32, (16, 256), 0)
 
-    def group_scores(r, h):
+    units = ((0, 0), (0, 1), (1, 0), (1, 1), (2, 0), (3, 0), (2, 1), (3, 1))
+
+    def correlate(unit):
+        r, h = units[unit]
         lanes = pl.ds(h * 256, 256)
-
-        def correlate(q, carry):
-            for k in range(OWN):
-                for std, lhs in ((std_hi, lhs_hi), (std_lo, lhs_lo)):
-                    line = jnp.broadcast_to(std[r * QUADS + q, pl.ds(k, 1), :], (16, 256))
-                    lhs[pl.ds(k * 16, 16), :] = jnp.where(own_row, line, 0.0).astype(BF16)
+        if r >= 2:
+            scales(r, h)
+        for q in range(QUADS):
+            at = r * QUADS + q
+            if h == 0:
+                for k in range(OWN):
+                    for std, lhs in ((std_hi, lhs_hi), (std_lo, lhs_lo)):
+                        line = jnp.broadcast_to(std[at, pl.ds(k, 1), :], (16, 256))
+                        lhs[at, pl.ds(k * 16, 16), :] = jnp.where(own_row, line, 0.0).astype(BF16)
             seen = epochs[r, q, :, lanes]
-            corr[q] = jnp.dot(lhs_hi[...], seen, preferred_element_type=F32) + jnp.dot(
-                lhs_lo[...], seen, preferred_element_type=F32
+            corr[unit % 2][q] = jnp.dot(lhs_hi[at], seen, preferred_element_type=F32) + jnp.dot(
+                lhs_lo[at], seen, preferred_element_type=F32
             )
-            return carry
-
-        lax.fori_loop(0, QUADS, correlate, 0)
-
-        def standard(k, carry):
-            rows = pl.ds(pl.multiple_of(k * 16, 16), 16)
+
+    def standard(unit):
+        r, h = units[unit]
+        lanes = pl.ds(h * 256, 256)
+        for k in range(OWN):
             halves = []
             for q in range(QUADS):
-                shrunk = corr[q, rows, :] * scale[r, q, :, lanes]
+                shrunk = corr[unit % 2][q, pl.ds(k * 16, 16), :] * scale[r, q, :, lanes]
                 twice = jnp.log(1.0 + shrunk) - jnp.log(1.0 - shrunk)
                 halves += [twice[0:8], twice[8:16]]
             mean = fold(functools.reduce(jnp.add, halves)) * (1.0 / EP)
@@ -335,82 +355,64 @@
                 score[k, pl.ds(at, 16), lanes] = both
                 if at < 64:
                     score[k, pl.ds(ROWS + at, 16), lanes] = both
-            return carry
-
-        lax.fori_loop(0, OWN, standard, 0, unroll=2)
-
-    with jax.named_scope("scores0"):
-        group_scores(0, 0)
-        group_scores(0, 1)
-    relay(0, 2)
-    with jax.named_scope("scores1"):
-        group_scores(1, 0)
-    relay(1, 0)
-    with jax.named_scope("scores1"):
-        group_scores(1, 1)
-    with jax.named_scope("scores2"):
-        scales(2, 0)
-        group_scores(2, 0)
-    relay(1, 1)
-    for q in range(QUADS):
-        relay_copy(0, q).wait_recv()
-    with jax.named_scope("scores3"):
-        scales(3, 0)
-        group_scores(3, 0)
-    relay(1, 2)
-    with jax.named_scope("scores4"):
-        scales(2, 1)
-        group_scores(2, 1)
-    for q in range(QUADS):
-        relay_copy(1, q).wait_recv()
-    with jax.named_scope("scores5"):
-        scales(3, 1)
-        group_scores(3, 1)
+
+    before = {
+        1: lambda: relay(0, 2),
+        2: lambda: relay(1, 0),
+        4: lambda: relay(1, 1),
+        5: lambda: [relay_copy(0, q).wait_recv() for q in range(QUADS)],
+        6: lambda: relay(1, 2),
+        7: lambda: [relay_copy(1, q).wait_recv() for q in range(QUADS)],
+    }
+    with jax.named_scope("scores"):
+        correlate(0)
+    for unit in range(1, len(units) + 1):
+        if unit in before:
+            before[unit]()
+        with jax.named_scope("scores"):
+            if unit < len(units):
+                correlate(unit)
+            standard(unit - 1)
 
     def block_of(m, block):
         gram[m, pl.ds(block * 64, 64), :] = lax.dot_general(
             score[m, pl.ds(block * 64, 64), :], score[m, pl.ds(block * 64, 128), :], NT, preferred_element_type=F32
         )
 
-    def kernels(step, carry):
-        major, minor = step // 4, step & 3
-        m = ahead_of(z, minor) * 4 + ahead_of(x, major)
-        block_of(m, 0)
-
-        @pl.when(minor == 0)
-        def _():
-            z_parts[major, 0] = gram[m, 0:64, :]
-
-        @pl.when(minor > 0)
-        def _():
-            to_v = shard_at(ahead_of(z, minor), x, y)
-            copy_to(gram.at[m, pl.ds(0, 64)], z_parts.at[major, minor], part_send, z_recv.at[major], j, to_v).start()
-
-        m = ahead_of(z, major) * 4 + ahead_of(x, minor)
-        block_of(m, 1)
-
-        @pl.when(minor == 0)
-        def _():
-            x_parts[major, 0] = gram[m, 64:128, :]
-
-        @pl.when(minor > 0)
-        def _():
-            to_v = shard_at(z, ahead_of(x, minor), y)
-            copy_to(gram.at[m, pl.ds(64, 64)], x_parts.at[major, minor], part_send, x_recv.at[major], j, to_v).start()
-
-        block_of(m, 2)
-        rows = pl.ds(pl.multiple_of(128 + 32 * (y ^ 1), 32), 32)
-        copy_to(gram.at[m, rows], y_parts.at[step], part_send, y_recv.at[major], j, v ^ 1).start()
+    def kernels(pair, carry):
+        steps = []
+        for step in (pair * 2, pair * 2 + 1):
+            major, minor = step // 4, step & 3
+            by_z = ahead_of(z, minor) * 4 + ahead_of(x, major)
+            by_x = ahead_of(z, major) * 4 + ahead_of(x, minor)
+            steps.append((step, major, minor, by_z, by_x))
+        for _, _, _, by_z, by_x in steps:
+            block_of(by_z, 0)
+            block_of(by_x, 1)
+            block_of(by_x, 2)
+        for step, major, minor, by_z, by_x in steps:
+
+            @pl.when(minor > 0)
+            def _():
+                to_v = shard_at(ahead_of(z, minor), x, y)
+                copy_to(gram.at[by_z, pl.ds(0, 64)], z_parts.at[major, minor], part_send, z_recv.at[major], j, to_v).start()
+                to_v = shard_at(z, ahead_of(x, minor), y)
+                copy_to(gram.at[by_x, pl.ds(64, 64)], x_parts.at[major, minor], part_send, x_recv.at[major], j, to_v).start()
+
+            rows = pl.ds(pl.multiple_of(128 + 32 * (y ^ 1), 32), 32)
+            copy_to(gram.at[by_x, rows], y_parts.at[step], part_send, y_recv.at[major], j, v ^ 1).start()
         return carry
 
     with jax.named_scope("kernels"):
-        lax.fori_loop(0, OWN, kernels, 0)
+        lax.fori_loop(0, OWN // 2, kernels, 0)
 
     for major in range(4):
         for block, parts, recv, sums in ((0, z_parts, z_recv, z_sums), (1, x_parts, x_recv, x_sums)):
             with jax.named_scope("part_wait"):
                 await_bytes(parts.at[major, pl.ds(1, 3)], recv.at[major])
-            sums[major] = (parts[major, 0] + parts[major, 1]) + (parts[major, 2] + parts[major, 3])
+            own = (ahead_of(z, major) * 4 + x) if block else (z * 4 + ahead_of(x, major))
+            own = gram[own, pl.ds(block * 64, 64), :]
+            sums[major] = (own + parts[major, 1]) + (parts[major, 2] + parts[major, 3])
             for other in range(2):
                 side = y ^ other
                 rows = pl.ds(pl.multiple_of(side * 32, 32), 32)
@@ -515,11 +517,13 @@
         out_shape=jax.ShapeDtypeStruct((2, EP * LOCAL, ROWS), F32),
         in_specs=[
             pl.BlockSpec(memory_space=pl.ANY),
-            pl.BlockSpec(memory_space=pltpu.SMEM),
-            pl.BlockSpec(memory_space=pltpu.SMEM),
+            pl.BlockSpec(memory_space=pl.ANY),
+            pl.BlockSpec(memory_space=pl.ANY),
         ],
         out_specs=pl.BlockSpec(memory_space=pltpu.VMEM),
         scratch_shapes=[
+            pltpu.SMEM((SUBJ * LOCAL, EP), I32),
+            pltpu.SMEM((SEL,), I32),
             vmem((LOCAL, RUN, VOX), BF16),
             vmem((QUADS * 256, LOCAL * RUN), BF16),
             vmem((SUBJ, QUADS, 256, VOX), BF16),
@@ -529,10 +533,11 @@
             vmem((2, QUADS * 256), BF16),
             vmem((SHARDS, 2, QUADS * 256), BF16),
             vmem((SUBJ * QUADS, OWN, 256), F32),
-            vmem((256, 256), BF16),
-            vmem((256, 256), BF16),
+            vmem((SUBJ * QUADS, 256, 256), BF16),
+            vmem((SUBJ * QUADS, 256, 256), BF16),
             vmem((SUBJ * QUADS, OWN, 256), F32),
             vmem((SUBJ * QUADS, OWN, 256), F32),
+            vmem((QUADS, 256, 256), F32),
             vmem((QUADS, 256, 256), F32),
             vmem((OWN, 256, VOX), BF16),
             vmem((OWN, ROWS, 128), F32),
@@ -548,7 +553,7 @@
             vmem((2, 3, EP * LOCAL, 64), BF16),
             vmem((2, 3, EP * LOCAL, 128), BF16),
             vmem((2, 3 * 128 + ROWS, ROWS), BF16),
-            dma,
+            dma((3,)),
             dma,
             dma,
             dma,

time: 60 us -> 58 us (0.967)
  Pallas kernels: 58.2 us -> 56.3 us
    pallas_call x1, Pallas kernels: 58.2 us -> 56.3 us  [body(): pl.pallas_call(main_kernel, out_shape=jax.ShapeDtypeStruct((2, EP * LOCAL...]
where the time goes in v3:
time: 58 us; the launch traced here: 57.8 us
  Pallas kernels  56.3 us (97%)
  local copies, waits for them, and re-layouts  1.54 us (3%)
    pallas_call x1, Pallas kernels, body(): pl.pallas_call(main_kernel, out_shape=jax.ShapeDtypeStruct((2, EP * LOCAL...  56.3 us
    unnamed x1, local copies, waits for them, and re-layouts  1.54 us

profile of v3, /device:TPU:1, one launch (start us, length us, event | category | flops | bytes accessed | tf_op | source)
XLA Modules:
  0.0 57.8 jit_solution(10674307689866664766)
XLA Ops:
  0.0 56.3 %shard_map.37 = f32[2,48,192]{2,1,0:T(8,128)} custom-call(bf16[4,256,512]{2,1,0:T(8,128)(2,1)} %series_hbm.1, s32[16,12]{1,0:T(8,128)} %offsets_hbm.1, s32[64]{0:T(128)} %selected_hbm.1), custom_call_target="tpu_custom_call" | custom-call | tf_op jit(solution)/shard_map/pallas_call | solution.py:515
  56.3 1.5 %copy.5 = f32[2,48,192]{2,1,0:T(8,128)} copy(f32[2,48,192]{2,1,0:T(8,128)} %shard_map.37) | data formatting | bytes 147456

commit v4 on v3

--- a/solution.py
+++ b/solution.py
@@ -50,8 +50,12 @@
     return first, second, (rest - second.astype(F32)).astype(BF16)
 
 
-def line_of(group, epoch, subject):
-    return group * (EP * LOCAL) + epoch * LOCAL + subject
+def slot_of(group, taker):
+    return jnp.where((group ^ taker) < 2, group ^ taker, 2 + (group & 1))
+
+
+def line_of(slot, epoch, subject):
+    return slot * (EP * LOCAL) + epoch * LOCAL + subject
 
 
 def main_kernel(
@@ -78,13 +82,18 @@
     corr_odd,
     score,
     gram,
-    z_parts,
-    x_parts,
+    z_parts_first,
+    z_parts_second,
+    x_parts_first,
+    x_parts_second,
     y_parts,
-    z_sums,
-    x_sums,
+    z_sums_first,
+    z_sums_second,
+    x_sums_first,
+    x_sums_second,
     y_sums,
-    last,
+    last_first,
+    last_second,
     total,
     final,
     pick_rows,
@@ -111,9 +120,14 @@
     final_recv,
 ):
     corr = (corr_even, corr_odd)
+    z_parts = (z_parts_first, z_parts_second)
+    x_parts = (x_parts_first, x_parts_second)
+    z_sums = (z_sums_first, z_sums_second)
+    x_sums = (x_sums_first, x_sums_second)
+    last = (last_first, last_second)
     j = lax.axis_index("subj")
     v = lax.axis_index("vox")
-    near, far = j ^ 1, j ^ 2
+    near, far, core = j ^ 1, j ^ 2, j & 1
     z, x, y = v // 8, (v // 2) & 3, v & 1
 
     def ahead_of(place, step):
@@ -203,25 +217,29 @@
     def near_copy(q):
         return copy_to(epochs.at[0, q], epochs.at[1, q], near_send.at[q], near_recv.at[q], near, v)
 
-    def half_of(r, h, q):
-        return epochs.at[r, q, :, pl.ds(h * 256, 256)]
-
-    def far_copy(h, q):
-        at = h * QUADS + q
-        return copy_to(half_of(0, h, q), half_of(2, h, q), far_send.at[at], far_recv.at[at], far, v)
-
-    def relay_copy(h, q):
-        at = h * QUADS + q
-        return copy_to(half_of(2, h, q), half_of(3, h, q), relay_send.at[at], relay_recv.at[at], near, v)
-
-    def relay(h, q):
+    half = pl.ds(pl.multiple_of(core * 256, 256), 256)
+
+    def far_copy(g, q):
+        at = g * QUADS + q
+        source, target = epochs.at[core ^ g, q, :, half], epochs.at[2 + g, q, :, half]
+        return copy_to(source, target, far_send.at[at], far_recv.at[at], far, v)
+
+    def relay_copy(g, q):
+        at = g * QUADS + q
+        ref = epochs.at[2 + g, q, :, half]
+        return copy_to(ref, ref, relay_send.at[at], relay_recv.at[at], near, v)
+
+    def relay(g, q):
         with jax.named_scope("relay"):
-            far_copy(h, q).wait_recv()
-            relay_copy(h, q).start()
+            far_copy(g, q).wait_recv()
+            relay_copy(g, q).start()
 
     for q in range(QUADS):
         near_copy(q).start()
-    far_copy(0, 0).start()
+
+    @pl.when(core == 0)
+    def _():
+        far_copy(0, 0).start()
 
     def scales(r, h):
         lanes = pl.ds(h * 256, 256)
@@ -233,6 +251,16 @@
     for h in range(2):
         scales(0, h)
 
+    with jax.named_scope("near_wait"):
+        for q in range(QUADS):
+            near_copy(q).wait_recv()
+
+    @pl.when(core == 1)
+    def _():
+        far_copy(0, 0).start()
+
+    far_copy(0, 1).start()
+
     own_group = v // 8 == j
 
     with jax.named_scope("slab_wait"):
@@ -257,7 +285,6 @@
         lax.fori_loop(1, SHARDS, share_slab, 0)
         slab[v] = slab_sum[...]
 
-    far_copy(0, 1).start()
     far_copy(0, 2).start()
     for q in range(QUADS):
         far_copy(1, q).start()
@@ -268,26 +295,25 @@
         for i in range(2):
             taker = y * 2 + i
             s = b // EP
-            to = line_of((s // LOCAL) ^ taker, b - s * EP, s & 3)
+            to = line_of(slot_of(s // LOCAL, taker), b - s * EP, s & 3)
             s = p // EP
-            line = line_of(j ^ taker, p - s * EP, s)
-            c = lax.broadcasted_iota(I32, (ROWS, 1), 0)
-            put_columns[i, pl.ds(3 * 128, ROWS), :] = jnp.where(c == to, 1.0, 0.0).astype(BF16)
-            for block in range(3):
-                c = lax.broadcasted_iota(I32, (128, 1), 0) + block * 64
-                c = jnp.where(c < ROWS, c, c - ROWS)
-                weight = jnp.where(lax.broadcasted_iota(I32, (128, ROWS), 0) < 64, 0.5, 1.0)
-                put_columns[i, pl.ds(block * 128, 128), :] = jnp.where(c == to, weight, 0.0).astype(BF16)
-                c = lax.broadcasted_iota(I32, (1, 128), 1) + block * 64
-                c = jnp.where(c < ROWS, c, c - ROWS)
-                weight = jnp.where(lax.broadcasted_iota(I32, (EP * LOCAL, 128), 1) < 64, 0.5, 1.0)
-                pick_turned[i, block] = jnp.where(c == line, weight, 0.0).astype(BF16)
-                c = lax.broadcasted_iota(I32, (1, 64), 1) + block * 64
-                pick_rows[i, block] = jnp.where(c == line, 1.0, 0.0).astype(BF16)
-
-    with jax.named_scope("near_wait"):
-        for q in range(QUADS):
-            near_copy(q).wait_recv()
+            line = line_of(slot_of(j, taker), p - s * EP, s)
+
+            def put(first, rows, lines):
+                put_columns[i, pl.ds(first, rows), :] = jnp.where(lines == to, 1.0, 0.0).astype(BF16)
+
+            across = lax.broadcasted_iota(I32, (1, 128), 1)
+            down = lax.broadcasted_iota(I32, (128, 1), 0)
+            for n in range(2):
+                put(n * 256, 128, down)
+                put(n * 256 + 128, 128, (down & 63) + (n + 1) * 64)
+                put(512 + n * 64, 64, lax.broadcasted_iota(I32, (64, 1), 0) + n * 128)
+                rows = lax.broadcasted_iota(I32, (1, 64), 1)
+                pick_rows[i, 2 * n] = jnp.where(rows + n * 128 == line, 1.0, 0.0).astype(BF16)
+                pick_rows[i, 2 * n + 1] = jnp.where(rows + (n + 1) * 64 == line, 1.0, 0.0).astype(BF16)
+                turned = across if n else jnp.where(across < 64, -1, across)
+                pick_turned[i, n] = jnp.where(turned == line, 1.0, 0.0).astype(BF16)
+
     for h in range(2):
         scales(1, h)
 
@@ -298,7 +324,7 @@
 
     with jax.named_scope("standard_slab"):
         for r in range(SUBJ):
-            group = (j ^ r) if r else j
+            group = (j, near, far & 2, far | 1)[r]
             for kk in range(8):
                 for q in range(QUADS):
                     raw[r * QUADS + q, pl.ds(kk * 2, 2), :] = slab[group * 8 + kk, :, pl.ds(q * 256, 256)].astype(F32)
@@ -317,7 +343,7 @@
 
     own_row = (lax.broadcasted_iota(I32, (16, 256), 1) & 15) == lax.broadcasted_iota(I32, (16, 256), 0)
 
-    units = ((0, 0), (0, 1), (1, 0), (1, 1), (2, 0), (3, 0), (2, 1), (3, 1))
+    units = ((0, 0), (0, 1), (1, 0), (1, 1), (2, 0), (2, 1), (3, 0), (3, 1))
 
     def correlate(unit):
         r, h = units[unit]
@@ -353,128 +379,204 @@
                 both = jnp.concatenate([halves[2 * q] * gain, halves[2 * q + 1] * gain], axis=0).astype(BF16)
                 at = r * 48 + q * 16
                 score[k, pl.ds(at, 16), lanes] = both
-                if at < 64:
-                    score[k, pl.ds(ROWS + at, 16), lanes] = both
-
-    before = {
-        1: lambda: relay(0, 2),
-        2: lambda: relay(1, 0),
-        4: lambda: relay(1, 1),
-        5: lambda: [relay_copy(0, q).wait_recv() for q in range(QUADS)],
-        6: lambda: relay(1, 2),
-        7: lambda: [relay_copy(1, q).wait_recv() for q in range(QUADS)],
-    }
-    with jax.named_scope("scores"):
-        correlate(0)
-    for unit in range(1, len(units) + 1):
-        if unit in before:
-            before[unit]()
-        with jax.named_scope("scores"):
-            if unit < len(units):
-                correlate(unit)
-            standard(unit - 1)
-
-    def block_of(m, block):
-        gram[m, pl.ds(block * 64, 64), :] = lax.dot_general(
-            score[m, pl.ds(block * 64, 64), :], score[m, pl.ds(block * 64, 128), :], NT, preferred_element_type=F32
+
+    split = ((48, 48, 0), (32, 32, 32))
+
+    def block_of(n, m):
+        top = pl.ds(n * 128, 64)
+        gram[n, m, 0:64, :] = lax.dot_general(
+            score[m, top, :], score[m, pl.ds(0, 128), :], NT, preferred_element_type=F32
         )
-
-    def kernels(pair, carry):
-        steps = []
-        for step in (pair * 2, pair * 2 + 1):
-            major, minor = step // 4, step & 3
-            by_z = ahead_of(z, minor) * 4 + ahead_of(x, major)
-            by_x = ahead_of(z, major) * 4 + ahead_of(x, minor)
-            steps.append((step, major, minor, by_z, by_x))
-        for _, _, _, by_z, by_x in steps:
-            block_of(by_z, 0)
-            block_of(by_x, 1)
-            block_of(by_x, 2)
-        for step, major, minor, by_z, by_x in steps:
-
-            @pl.when(minor > 0)
-            def _():
-                to_v = shard_at(ahead_of(z, minor), x, y)
-                copy_to(gram.at[by_z, pl.ds(0, 64)], z_parts.at[major, minor], part_send, z_recv.at[major], j, to_v).start()
-                to_v = shard_at(z, ahead_of(x, minor), y)
-                copy_to(gram.at[by_x, pl.ds(64, 64)], x_parts.at[major, minor], part_send, x_recv.at[major], j, to_v).start()
-
-            rows = pl.ds(pl.multiple_of(128 + 32 * (y ^ 1), 32), 32)
-            copy_to(gram.at[by_x, rows], y_parts.at[step], part_send, y_recv.at[major], j, v ^ 1).start()
-        return carry
-
-    with jax.named_scope("kernels"):
-        lax.fori_loop(0, OWN // 2, kernels, 0)
-
-    for major in range(4):
-        for block, parts, recv, sums in ((0, z_parts, z_recv, z_sums), (1, x_parts, x_recv, x_sums)):
+        rows = score[m, pl.ds((n + 1) * 64, 64), :]
+        square = lax.dot_general(rows, rows, NT, preferred_element_type=F32)
+        gram[n, m, 64:96, :] = jnp.concatenate([square[0:32], square[32:64]], axis=1)
+
+    def kernels(n):
+        z_rows, x_rows, y_rows = split[n]
+
+        def pair(index, carry):
+            for step in (index * 2, index * 2 + 1):
+                block_of(n, ahead_of(z, step // 4) * 4 + ahead_of(x, step & 3))
+            for step in (index * 2, index * 2 + 1):
+                major, minor = step // 4, step & 3
+                m = ahead_of(z, major) * 4 + ahead_of(x, minor)
+
+                @pl.when(major > 0)
+                def _():
+                    source = gram.at[n, m, pl.ds(0, z_rows)]
+                    to_v = shard_at(ahead_of(z, major), x, y)
+                    copy_to(source, z_parts[n].at[minor, major], part_send.at[n], z_recv.at[n, minor], j, to_v).start()
+
+                @pl.when(minor > 0)
+                def _():
+                    source = gram.at[n, m, pl.ds(z_rows, x_rows)]
+                    to_v = shard_at(z, ahead_of(x, minor), y)
+                    copy_to(source, x_parts[n].at[major, minor], part_send.at[n], x_recv.at[n, major], j, to_v).start()
+
+                if y_rows:
+                    rows = pl.ds(pl.multiple_of(z_rows + x_rows + y_rows // 2 * (y ^ 1), 8), y_rows // 2)
+                    copy_to(
+                        gram.at[n, m, rows], y_parts.at[step], part_send.at[n], y_recv.at[major], j, v ^ 1
+                    ).start()
+            return carry
+
+        with jax.named_scope("kernels"):
+            lax.fori_loop(0, OWN // 2, pair, 0)
+
+    def second_sums(n):
+        z_rows, x_rows, y_rows = split[n]
+
+        def along(step, block):
+            parts, recv, sums = ((z_parts, z_recv, z_sums), (x_parts, x_recv, x_sums))[block]
             with jax.named_scope("part_wait"):
-                await_bytes(parts.at[major, pl.ds(1, 3)], recv.at[major])
-            own = (ahead_of(z, major) * 4 + x) if block else (z * 4 + ahead_of(x, major))
-            own = gram[own, pl.ds(block * 64, 64), :]
-            sums[major] = (own + parts[major, 1]) + (parts[major, 2] + parts[major, 3])
+                await_bytes(parts[n].at[step, pl.ds(1, 3)], recv.at[n, step])
+            own = (ahead_of(z, step) * 4 + x) if block else (z * 4 + ahead_of(x, step))
+            own = gram[n, own, pl.ds(z_rows, x_rows) if block else pl.ds(0, z_rows), :]
+            sums[n][step] = (own + parts[n][step, 1]) + (parts[n][step, 2] + parts[n][step, 3])
             for other in range(2):
                 side = y ^ other
-                rows = pl.ds(pl.multiple_of(side * 32, 32), 32)
-                slot = major * 2 + other
-                to_v = shard_at(ahead_of(z, major), x, side) if block else shard_at(z, ahead_of(x, major), side)
+                count = (z_rows, x_rows)[block] // 2
+                rows = pl.ds(pl.multiple_of(side * count, 8), count)
+                slot = step * 2 + other
+                to_v = shard_at(ahead_of(z, step), x, side) if block else shard_at(z, ahead_of(x, step), side)
                 if slot:
-                    copy_to(sums.at[major, rows], last.at[block * 8 + slot], sum_send, sum_recv, j, to_v).start()
+                    copy_to(
+                        sums[n].at[step, rows], last[n].at[block * 8 + slot], sum_send.at[n], sum_recv.at[n], j, to_v
+                    ).start()
                 else:
-                    last[block * 8] = sums[0, rows, :]
-        with jax.named_scope("part_wait"):
-            await_bytes(y_parts.at[pl.ds(major * 4, 4)], y_recv.at[major])
-        for minor in range(4):
-            step = major * 4 + minor
-            to_z, to_x = ahead_of(z, major), ahead_of(x, minor)
-            rows = pl.ds(pl.multiple_of(128 + 32 * y, 32), 32)
-            added = y_parts[step] + gram[to_z * 4 + to_x, rows, :]
-            if step:
-                y_sums[step] = added
-                copy_to(y_sums.at[step], last.at[16 + step], sum_send, sum_recv, j, shard_at(to_z, to_x, y)).start()
-            else:
-                last[16] = added
-
-    with jax.named_scope("last_wait"):
-        await_bytes(last.at[pl.ds(0, 29)], sum_recv)
-
-    mean = 1.0 / (VOX * SHARDS)
-    total[0:32, :] = jnp.sum(last[0:8], axis=0) * mean
-    total[32:64, :] = jnp.sum(last[8:16], axis=0) * mean
-    total[64:96, :] = jnp.sum(last[16:32], axis=0) * mean
+                    last[n][block * 8] = sums[n][0, rows, :]
+
+        def from_side(major):
+            with jax.named_scope("part_wait"):
+                await_bytes(y_parts.at[pl.ds(major * 4, 4)], y_recv.at[major])
+            for minor in range(4):
+                step = major * 4 + minor
+                to_z, to_x = ahead_of(z, major), ahead_of(x, minor)
+                rows = pl.ds(pl.multiple_of(z_rows + x_rows + y_rows // 2 * y, 8), y_rows // 2)
+                added = y_parts[step] + gram[n, to_z * 4 + to_x, rows, :]
+                if step:
+                    y_sums[step] = added
+                    copy_to(
+                        y_sums.at[step], last[n].at[16 + step], sum_send.at[n], sum_recv.at[n], j, shard_at(to_z, to_x, y)
+                    ).start()
+                else:
+                    last[n][16] = added
+
+        if y_rows:
+            for major in range(4):
+                along(major, 1)
+                from_side(major)
+            for step in range(4):
+                along(step, 0)
+        else:
+            for step in range(4):
+                along(step, 1)
+            for step in range(4):
+                along(step, 0)
 
     owner_v = v - y + j // 2
-    place = (j & 1) * 2 + y
-    with jax.named_scope("final"):
+    place = core * 2 + y
+    remote_sums = (14, 29)
+
+    def hand_over(n):
+        with jax.named_scope("last_wait"):
+            await_bytes(last[n].at[pl.ds(0, remote_sums[n])], sum_recv.at[n])
+        mean = 1.0 / (VOX * SHARDS)
+        first = 0
+        for block, rows in enumerate(split[n]):
+            if rows:
+                slots = last[n][block * 8 : (block + (2 if block == 2 else 1)) * 8]
+                total[n, pl.ds(first, rows // 2), :] = jnp.sum(slots, axis=0) * mean
+                first += rows // 2
         for other in range(SUBJ):
-            to_j = (j ^ other) if other else j
+            copy = copy_to(
+                total.at[n], final.at[n, place], final_send.at[n], final_recv.at[n], (j ^ other) if other else j, owner_v
+            )
             if other:
-                copy_to(total, final.at[place], final_send, final_recv, to_j, owner_v).start()
+                copy.start()
             else:
 
                 @pl.when(owner_v != v)
                 def _():
-                    copy_to(total, final.at[place], final_send, final_recv, j, owner_v).start()
+                    copy.start()
 
         @pl.when(owner_v == v)
         def _():
-            final[place] = total[...]
-            await_bytes(final.at[pl.ds(0, SUBJ - 1)], final_recv)
+            final[n, place] = total[n]
+
+    def await_final(n, sem):
+        @pl.when(owner_v == v)
+        def _():
+            await_bytes(final.at[n, pl.ds(0, SUBJ - 1)], sem.at[n])
 
         @pl.when(owner_v != v)
         def _():
-            await_bytes(final, final_recv)
+            await_bytes(final.at[n], sem.at[n])
+
+    def scores_of(correlated, finished):
+        with jax.named_scope("scores"):
+            if correlated is not None:
+                correlate(correlated)
+            if finished is not None:
+                standard(finished)
+
+    def relayed(g):
+        with jax.named_scope("relay_wait"):
+            for q in range(QUADS):
+                relay_copy(g, q).wait_recv()
+
+    scores_of(0, None)
+    scores_of(1, 0)
+    relay(0, 2)
+    scores_of(2, 1)
+    scores_of(3, 2)
+    relayed(0)
+    scores_of(4, 3)
+    scores_of(5, 4)
+    scores_of(None, 5)
+    relay(1, 0)
+    kernels(0)
+    relay(1, 1)
+    relay(1, 2)
+    relayed(1)
+    scores_of(6, None)
+    scores_of(7, 6)
+    scores_of(None, 7)
+    kernels(1)
+    second_sums(0)
+    second_sums(1)
+    hand_over(0)
+    hand_over(1)
+    with jax.named_scope("final"):
+        await_final(0, final_recv)
+        await_final(1, final_recv)
 
     with jax.named_scope("place"):
+        beside = lax.broadcasted_iota(I32, (EP * LOCAL, 128), 1) < 64
+
+        def picked_by(pick, terms, dims):
+            parts = [lax.dot_general(pick, t, dims, preferred_element_type=F32) for t in terms]
+            return parts[0] + parts[1] + parts[2]
+
         for i in range(2):
-            taken = []
-            for block in range(3):
-                rows = pl.ds(block * 32, 32)
-                terms = exact_terms(jnp.concatenate([final[2 * i, rows, :], final[2 * i + 1, rows, :]], axis=0))
-                wide = [jnp.dot(pick_rows[i, block], t, preferred_element_type=F32) for t in terms]
-                tall = [lax.dot_general(pick_turned[i, block], t, NT, preferred_element_type=F32) for t in terms]
-                taken.append((wide[0] + wide[1] + wide[2], tall[0] + tall[1] + tall[2]))
-            lines = jnp.concatenate([t[0] for t in taken] + [t[1] for t in taken], axis=1)
+            lines, turned = [], []
+            for n in range(2):
+                pieces, first = [], 0
+                for rows in split[n]:
+                    if rows:
+                        here = pl.ds(first, rows // 2)
+                        pieces += [final[n, 2 * i, here, :], final[n, 2 * i + 1, here, :]]
+                        first += rows // 2
+                both = jnp.concatenate(pieces, axis=0)
+                wide, square = exact_terms(both[0:64]), exact_terms(both[64:96])
+                lines.append(picked_by(pick_rows[i, 2 * n], wide, (((1,), (0,)), ((), ()))))
+                halves = [
+                    picked_by(pick_rows[i, 2 * n + 1, :, h * 32 : h * 32 + 32], square, (((1,), (0,)), ((), ())))
+                    for h in range(2)
+                ]
+                lines.append(jnp.where(beside, halves[0], halves[1]))
+                turned.append(picked_by(pick_turned[i, n], wide, NT))
+            lines = jnp.concatenate(lines + turned, axis=1)
             terms = [jnp.dot(t, put_columns[i], preferred_element_type=F32) for t in exact_terms(lines)]
             out_ref[i] = terms[0] + terms[1] + terms[2]
 
@@ -489,19 +591,12 @@
         def _():
             await_bytes(slab_in, slab_send)
 
-        for _ in range(2):
-            await_bytes(z_parts.at[pl.ds(0, 3)], part_send)
-        await_bytes(y_parts, part_send)
-        await_bytes(last.at[pl.ds(0, 29)], sum_send)
-
-        @pl.when(owner_v == v)
-        def _():
-            await_bytes(final.at[pl.ds(0, SUBJ - 1)], final_send)
-
-        @pl.when(owner_v != v)
-        def _():
-            await_bytes(final, final_send)
-
+        for n in range(2):
+            await_bytes(z_parts[n].at[pl.ds(0, 3)], part_send.at[n])
+            await_bytes(x_parts[n].at[pl.ds(0, 3)], part_send.at[n])
+            await_bytes(last[n].at[pl.ds(0, remote_sums[n])], sum_send.at[n])
+            await_final(n, final_send)
+        await_bytes(y_parts, part_send.at[1])
         for q in range(QUADS):
             near_copy(q).wait_send()
             for h in range(2):
@@ -539,20 +634,25 @@
             vmem((SUBJ * QUADS, OWN, 256), F32),
             vmem((QUADS, 256, 256), F32),
             vmem((QUADS, 256, 256), F32),
-            vmem((OWN, 256, VOX), BF16),
-            vmem((OWN, ROWS, 128), F32),
-            vmem((4, 4, 64, 128), F32),
-            vmem((4, 4, 64, 128), F32),
-            vmem((OWN, 32, 128), F32),
-            vmem((4, 64, 128), F32),
-            vmem((4, 64, 128), F32),
-            vmem((OWN, 32, 128), F32),
-            vmem((32, 32, 128), F32),
-            vmem((96, 128), F32),
-            vmem((SUBJ, 96, 128), F32),
-            vmem((2, 3, EP * LOCAL, 64), BF16),
-            vmem((2, 3, EP * LOCAL, 128), BF16),
-            vmem((2, 3 * 128 + ROWS, ROWS), BF16),
+            vmem((OWN, ROWS, VOX), BF16),
+            vmem((2, OWN, 96, 128), F32),
+            vmem((4, 4, 48, 128), F32),
+            vmem((4, 4, 32, 128), F32),
+            vmem((4, 4, 48, 128), F32),
+            vmem((4, 4, 32, 128), F32),
+            vmem((OWN, 16, 128), F32),
+            vmem((4, 48, 128), F32),
+            vmem((4, 32, 128), F32),
+            vmem((4, 48, 128), F32),
+            vmem((4, 32, 128), F32),
+            vmem((OWN, 16, 128), F32),
+            vmem((16, 24, 128), F32),
+            vmem((32, 16, 128), F32),
+            vmem((2, 48, 128), F32),
+            vmem((2, SUBJ, 48, 128), F32),
+            vmem((2, 4, EP * LOCAL, 64), BF16),
+            vmem((2, 2, EP * LOCAL, 128), BF16),
+            vmem((2, 5 * 128, ROWS), BF16),
             dma((3,)),
             dma,
             dma,
@@ -564,14 +664,14 @@
             dma((2 * QUADS,)),
             dma((2 * QUADS,)),
             dma((2 * QUADS,)),
-            dma,
+            dma((2,)),
+            dma((2, 4)),
+            dma((2, 4)),
             dma((4,)),
-            dma((4,)),
-            dma((4,)),
-            dma,
-            dma,
-            dma,
-            dma,
+            dma((2,)),
+            dma((2,)),
+            dma((2,)),
+            dma((2,)),
         ],
         compiler_params=pltpu.CompilerParams(collective_id=0, has_side_effects=True),
     )(series, offsets, selected)

time: 58 us -> 52.6 us (0.907)
  Pallas kernels: 56.3 us -> 50.9 us
    pallas_call x1, Pallas kernels: 56.3 us -> 50.9 us  [body(): pl.pallas_call(main_kernel, out_shape=jax.ShapeDtypeStruct((2, EP * LOCAL...]
where the time goes in v4:
time: 52.6 us; the launch traced here: 52.4 us
  Pallas kernels  50.9 us (97%)
  local copies, waits for them, and re-layouts  1.54 us (3%)
    pallas_call x1, Pallas kernels, body(): pl.pallas_call(main_kernel, out_shape=jax.ShapeDtypeStruct((2, EP * LOCAL...  50.9 us
    unnamed x1, local copies, waits for them, and re-layouts  1.54 us

profile of v4, /device:TPU:1, one launch (start us, length us, event | category | flops | bytes accessed | tf_op | source)
XLA Modules:
  0.0 52.4 jit_solution(6409671657655772520)
XLA Ops:
  0.0 50.9 %shard_map.37 = f32[2,48,192]{2,1,0:T(8,128)} custom-call(bf16[4,256,512]{2,1,0:T(8,128)(2,1)} %series_hbm.1, s32[16,12]{1,0:T(8,128)} %offsets_hbm.1, s32[64]{0:T(128)} %selected_hbm.1), custom_call_target="tpu_custom_call" | custom-call | tf_op jit(solution)/shard_map/pallas_call | solution.py:610
  50.9 1.5 %copy.5 = f32[2,48,192]{2,1,0:T(8,128)} copy(f32[2,48,192]{2,1,0:T(8,128)} %shard_map.37) | data formatting | bytes 147456

commit v5 on v4

--- a/solution.py
+++ b/solution.py
@@ -148,17 +148,15 @@
     barrier = pltpu.get_barrier_semaphore()
 
     def greet(step, carry):
+        to = step ^ 21
+        to_v = shard_at(ahead_of(z, to // 8), ahead_of(x, (to // 2) & 3), y ^ (to & 1))
         for other in range(SUBJ):
-            pl.semaphore_signal(
-                barrier,
-                inc=1,
-                device_id={"subj": j ^ other, "vox": (v + step) & (SHARDS - 1)},
-                device_id_type=MESH,
-            )
+            pl.semaphore_signal(barrier, inc=1, device_id={"subj": j ^ other, "vox": to_v}, device_id_type=MESH)
         return carry
 
     with jax.named_scope("greet"):
-        lax.fori_loop(1, SHARDS, greet, 0, unroll=4)
+        lax.fori_loop(0, 21, greet, 0, unroll=3)
+        lax.fori_loop(22, SHARDS, greet, 0, unroll=2)
         for other in range(1, SUBJ):
             pl.semaphore_signal(barrier, inc=1, device_id={"subj": j ^ other, "vox": v}, device_id_type=MESH)
 
@@ -305,9 +303,9 @@
             across = lax.broadcasted_iota(I32, (1, 128), 1)
             down = lax.broadcasted_iota(I32, (128, 1), 0)
             for n in range(2):
-                put(n * 256, 128, down)
-                put(n * 256 + 128, 128, (down & 63) + (n + 1) * 64)
-                put(512 + n * 64, 64, lax.broadcasted_iota(I32, (64, 1), 0) + n * 128)
+                put(n * 320, 128, down)
+                put(n * 320 + 128, 128, (down & 63) + (n + 1) * 64)
+                put(n * 320 + 256, 64, lax.broadcasted_iota(I32, (64, 1), 0) + n * 128)
                 rows = lax.broadcasted_iota(I32, (1, 64), 1)
                 pick_rows[i, 2 * n] = jnp.where(rows + n * 128 == line, 1.0, 0.0).astype(BF16)
                 pick_rows[i, 2 * n + 1] = jnp.where(rows + (n + 1) * 64 == line, 1.0, 0.0).astype(BF16)
@@ -362,13 +360,14 @@
                 lhs_lo[at], seen, preferred_element_type=F32
             )
 
-    def standard(unit):
+    def standard(unit, ids=range(OWN)):
         r, h = units[unit]
         lanes = pl.ds(h * 256, 256)
-        for k in range(OWN):
+        for k in ids:
+            rows = pl.ds(k * 16 if isinstance(k, int) else pl.multiple_of(k * 16, 16), 16)
             halves = []
             for q in range(QUADS):
-                shrunk = corr[unit % 2][q, pl.ds(k * 16, 16), :] * scale[r, q, :, lanes]
+                shrunk = corr[unit % 2][q, rows, :] * scale[r, q, :, lanes]
                 twice = jnp.log(1.0 + shrunk) - jnp.log(1.0 - shrunk)
                 halves += [twice[0:8], twice[8:16]]
             mean = fold(functools.reduce(jnp.add, halves)) * (1.0 / EP)
@@ -391,12 +390,17 @@
         square = lax.dot_general(rows, rows, NT, preferred_element_type=F32)
         gram[n, m, 64:96, :] = jnp.concatenate([square[0:32], square[32:64]], axis=1)
 
-    def kernels(n):
+    def kernels(n, unfinished=None):
         z_rows, x_rows, y_rows = split[n]
+
+        def id_at(step):
+            return ahead_of(z, step // 4) * 4 + ahead_of(x, step & 3)
 
         def pair(index, carry):
             for step in (index * 2, index * 2 + 1):
-                block_of(n, ahead_of(z, step // 4) * 4 + ahead_of(x, step & 3))
+                block_of(n, id_at(step))
+            if unfinished is not None:
+                standard(unfinished, [id_at((index * 2 + more) & 15) for more in (2, 3)])
             for step in (index * 2, index * 2 + 1):
                 major, minor = step // 4, step & 3
                 m = ahead_of(z, major) * 4 + ahead_of(x, minor)
@@ -421,6 +425,8 @@
             return carry
 
         with jax.named_scope("kernels"):
+            if unfinished is not None:
+                standard(unfinished, [id_at(0), id_at(1)])
             lax.fori_loop(0, OWN // 2, pair, 0)
 
     def second_sums(n):
@@ -538,47 +544,53 @@
     kernels(0)
     relay(1, 1)
     relay(1, 2)
+    second_sums(0)
     relayed(1)
     scores_of(6, None)
     scores_of(7, 6)
-    scores_of(None, 7)
-    kernels(1)
-    second_sums(0)
+    kernels(1, 7)
     second_sums(1)
     hand_over(0)
     hand_over(1)
+
+    beside = lax.broadcasted_iota(I32, (EP * LOCAL, 128), 1) < 64
+
+    def picked_by(pick, terms, dims):
+        parts = [lax.dot_general(pick, t, dims, preferred_element_type=F32) for t in terms]
+        return parts[0] + parts[1] + parts[2]
+
+    def placed(n, i):
+        pieces, first = [], 0
+        for rows in split[n]:
+            if rows:
+                here = pl.ds(first, rows // 2)
+                pieces += [final[n, 2 * i, here, :], final[n, 2 * i + 1, here, :]]
+                first += rows // 2
+        both = jnp.concatenate(pieces, axis=0)
+        wide, square = exact_terms(both[0:64]), exact_terms(both[64:96])
+        halves = [
+            picked_by(pick_rows[i, 2 * n + 1, :, h * 32 : h * 32 + 32], square, (((1,), (0,)), ((), ())))
+            for h in range(2)
+        ]
+        lines = [
+            picked_by(pick_rows[i, 2 * n], wide, (((1,), (0,)), ((), ()))),
+            jnp.where(beside, halves[0], halves[1]),
+            picked_by(pick_turned[i, n], wide, NT),
+        ]
+        put = put_columns[i, pl.ds(n * 320, 320), :]
+        terms = [jnp.dot(t, put, preferred_element_type=F32) for t in exact_terms(jnp.concatenate(lines, axis=1))]
+        return terms[0] + terms[1] + terms[2]
+
     with jax.named_scope("final"):
         await_final(0, final_recv)
+    with jax.named_scope("place"):
+        for i in range(2):
+            out_ref[i] = placed(0, i)
+    with jax.named_scope("final"):
         await_final(1, final_recv)
-
     with jax.named_scope("place"):
-        beside = lax.broadcasted_iota(I32, (EP * LOCAL, 128), 1) < 64
-
-        def picked_by(pick, terms, dims):
-            parts = [lax.dot_general(pick, t, dims, preferred_element_type=F32) for t in terms]
-            return parts[0] + parts[1] + parts[2]
-
         for i in range(2):
-            lines, turned = [], []
-            for n in range(2):
-                pieces, first = [], 0
-                for rows in split[n]:
-                    if rows:
-                        here = pl.ds(first, rows // 2)
-                        pieces += [final[n, 2 * i, here, :], final[n, 2 * i + 1, here, :]]
-                        first += rows // 2
-                both = jnp.concatenate(pieces, axis=0)
-                wide, square = exact_terms(both[0:64]), exact_terms(both[64:96])
-                lines.append(picked_by(pick_rows[i, 2 * n], wide, (((1,), (0,)), ((), ()))))
-                halves = [
-                    picked_by(pick_rows[i, 2 * n + 1, :, h * 32 : h * 32 + 32], square, (((1,), (0,)), ((), ())))
-                    for h in range(2)
-                ]
-                lines.append(jnp.where(beside, halves[0], halves[1]))
-                turned.append(picked_by(pick_turned[i, n], wide, NT))
-            lines = jnp.concatenate(lines + turned, axis=1)
-            terms = [jnp.dot(t, put_columns[i], preferred_element_type=F32) for t in exact_terms(lines)]
-            out_ref[i] = terms[0] + terms[1] + terms[2]
+            out_ref[i] += placed(1, i)
 
     with jax.named_scope("drain"):
         await_bytes(slab_in.at[pl.ds(0, SHARDS - 1)], share_send)
@@ -609,7 +621,7 @@
     dma = pltpu.SemaphoreType.DMA
     return pl.pallas_call(
         main_kernel,
-        out_shape=jax.ShapeDtypeStruct((2, EP * LOCAL, ROWS), F32),
+        out_shape=pltpu.VMEM((2, EP * LOCAL, ROWS), F32),
         in_specs=[
             pl.BlockSpec(memory_space=pl.ANY),
             pl.BlockSpec(memory_space=pl.ANY),

time: 52.6 us -> 53 us (level)
  Pallas kernels: 50.9 us -> 52.3 us
  local copies, waits for them, and re-layouts: 1.54 us -> 0.64 us
    pallas_call x1, Pallas kernels: 50.9 us -> 52.3 us  [body(): pl.pallas_call(main_kernel, out_shape=pltpu.VMEM((2, EP * LOCAL, ROWS), F...]
    unnamed x1, local copies, waits for them, and re-layouts: 1.54 us -> 0.64 us
where the time goes in v5:
time: 53 us; the launch traced here: 52.9 us
  Pallas kernels  52.3 us (99%)
  local copies, waits for them, and re-layouts  0.64 us (1%)
    pallas_call x1, Pallas kernels, body(): pl.pallas_call(main_kernel, out_shape=pltpu.VMEM((2, EP * LOCAL, ROWS), F...  52.3 us

profile of v5, /device:TPU:1, one launch (start us, length us, event | category | flops | bytes accessed | tf_op | source)
XLA Modules:
  0.0 52.9 jit_solution(6151892559556444257)
XLA Ops:
  0.0 52.3 %shard_map.37 = f32[2,48,192]{2,1,0:T(8,128)S(1)} custom-call(bf16[4,256,512]{2,1,0:T(8,128)(2,1)} %series_hbm.1, s32[16,12]{1,0:T(8,128)} %offsets_hbm.1, s32[64]{0:T(128)} %selected_hbm.1), custom_call_target="tpu_custom_call" | custom-call | tf_op jit(solution)/shard_map/pallas_call | solution.py:622
  52.3 0.6 %copy.5 = f32[2,48,192]{2,1,0:T(8,128)} copy(f32[2,48,192]{2,1,0:T(8,128)S(1)} %shard_map.37) | data formatting | bytes 147456

commit v6 on v5

--- a/solution.py
+++ b/solution.py
@@ -148,15 +148,17 @@
     barrier = pltpu.get_barrier_semaphore()
 
     def greet(step, carry):
-        to = step ^ 21
-        to_v = shard_at(ahead_of(z, to // 8), ahead_of(x, (to // 2) & 3), y ^ (to & 1))
         for other in range(SUBJ):
-            pl.semaphore_signal(barrier, inc=1, device_id={"subj": j ^ other, "vox": to_v}, device_id_type=MESH)
+            pl.semaphore_signal(
+                barrier,
+                inc=1,
+                device_id={"subj": j ^ other, "vox": (v + step) & (SHARDS - 1)},
+                device_id_type=MESH,
+            )
         return carry
 
     with jax.named_scope("greet"):
-        lax.fori_loop(0, 21, greet, 0, unroll=3)
-        lax.fori_loop(22, SHARDS, greet, 0, unroll=2)
+        lax.fori_loop(1, SHARDS, greet, 0, unroll=4)
         for other in range(1, SUBJ):
             pl.semaphore_signal(barrier, inc=1, device_id={"subj": j ^ other, "vox": v}, device_id_type=MESH)
 
@@ -319,6 +321,7 @@
     relay(0, 1)
     with jax.named_scope("share_wait"):
         await_bytes(slab.at[pl.ds(0, SHARDS - 1)], share_recv)
+    relay(0, 2)
 
     with jax.named_scope("standard_slab"):
         for r in range(SUBJ):
@@ -396,12 +399,13 @@
         def id_at(step):
             return ahead_of(z, step // 4) * 4 + ahead_of(x, step & 3)
 
-        def pair(index, carry):
-            for step in (index * 2, index * 2 + 1):
+        def four(index, carry):
+            steps = [index * 4 + more for more in range(8)]
+            for step in steps[:4]:
                 block_of(n, id_at(step))
             if unfinished is not None:
-                standard(unfinished, [id_at((index * 2 + more) & 15) for more in (2, 3)])
-            for step in (index * 2, index * 2 + 1):
+                standard(unfinished, [id_at(step & 15) for step in steps[4:]])
+            for step in steps[:4]:
                 major, minor = step // 4, step & 3
                 m = ahead_of(z, major) * 4 + ahead_of(x, minor)
 
@@ -426,8 +430,8 @@
 
         with jax.named_scope("kernels"):
             if unfinished is not None:
-                standard(unfinished, [id_at(0), id_at(1)])
-            lax.fori_loop(0, OWN // 2, pair, 0)
+                standard(unfinished, [id_at(step) for step in range(4)])
+            lax.fori_loop(0, OWN // 4, four, 0)
 
     def second_sums(n):
         z_rows, x_rows, y_rows = split[n]
@@ -533,22 +537,21 @@
 
     scores_of(0, None)
     scores_of(1, 0)
-    relay(0, 2)
     scores_of(2, 1)
     scores_of(3, 2)
     relayed(0)
     scores_of(4, 3)
+    relay(1, 0)
     scores_of(5, 4)
     scores_of(None, 5)
-    relay(1, 0)
+    relay(1, 1)
     kernels(0)
-    relay(1, 1)
     relay(1, 2)
-    second_sums(0)
     relayed(1)
     scores_of(6, None)
     scores_of(7, 6)
     kernels(1, 7)
+    second_sums(0)
     second_sums(1)
     hand_over(0)
     hand_over(1)

time: 53 us -> 50.3 us (0.949)
  Pallas kernels: 52.3 us -> 49.5 us
    pallas_call x1, Pallas kernels: 52.3 us -> 49.5 us  [body(): pl.pallas_call(main_kernel, out_shape=pltpu.VMEM((2, EP * LOCAL, ROWS), F...]
where the time goes in v6:
time: 50.3 us; the launch traced here: 50.2 us
  Pallas kernels  49.5 us (98%)
  local copies, waits for them, and re-layouts  0.64 us (1%)
    pallas_call x1, Pallas kernels, body(): pl.pallas_call(main_kernel, out_shape=pltpu.VMEM((2, EP * LOCAL, ROWS), F...  49.5 us

profile of v6, /device:TPU:1, one launch (start us, length us, event | category | flops | bytes accessed | tf_op | source)
XLA Modules:
  0.0 50.2 jit_solution(15760861557926696318)
XLA Ops:
  0.0 49.5 %shard_map.37 = f32[2,48,192]{2,1,0:T(8,128)S(1)} custom-call(bf16[4,256,512]{2,1,0:T(8,128)(2,1)} %series_hbm.1, s32[16,12]{1,0:T(8,128)} %offsets_hbm.1, s32[64]{0:T(128)} %selected_hbm.1), custom_call_target="tpu_custom_call" | custom-call | tf_op jit(solution)/shard_map/pallas_call | solution.py:625
  49.5 0.6 %copy.5 = f32[2,48,192]{2,1,0:T(8,128)} copy(f32[2,48,192]{2,1,0:T(8,128)S(1)} %shard_map.37) | data formatting | bytes 147456

commit v7 on v6

--- a/solution.py
+++ b/solution.py
@@ -48,6 +48,11 @@
     rest = x - first.astype(F32)
     second = rest.astype(BF16)
     return first, second, (rest - second.astype(F32)).astype(BF16)
+
+
+def two_terms(x):
+    first = x.astype(BF16)
+    return first, (x - first.astype(F32)).astype(BF16)
 
 
 def slot_of(group, taker):
@@ -81,23 +86,43 @@
     corr_even,
     corr_odd,
     score,
-    gram,
-    z_parts_first,
-    z_parts_second,
-    x_parts_first,
-    x_parts_second,
+    gram_a,
+    gram_b,
+    gram_c,
+    z_parts_a,
+    z_parts_b,
+    z_parts_c,
+    x_parts_a,
+    x_parts_b,
+    x_parts_c,
     y_parts,
-    z_sums_first,
-    z_sums_second,
-    x_sums_first,
-    x_sums_second,
+    z_sums_a,
+    z_sums_b,
+    z_sums_c,
+    x_sums_a,
+    x_sums_b,
+    x_sums_c,
     y_sums,
-    last_first,
-    last_second,
-    total,
-    final,
-    pick_rows,
-    pick_turned,
+    z_last_a,
+    z_last_b,
+    z_last_c,
+    x_last_a,
+    x_last_b,
+    x_last_c,
+    y_last,
+    total_a,
+    total_b,
+    total_c,
+    final_a,
+    final_b,
+    final_c,
+    pick_a,
+    pick_b,
+    pick_wide,
+    pick_square,
+    turn_a,
+    turn_b,
+    turn_c,
     put_columns,
     load_sem,
     slab_send,
@@ -120,11 +145,11 @@
     final_recv,
 ):
     corr = (corr_even, corr_odd)
-    z_parts = (z_parts_first, z_parts_second)
-    x_parts = (x_parts_first, x_parts_second)
-    z_sums = (z_sums_first, z_sums_second)
-    x_sums = (x_sums_first, x_sums_second)
-    last = (last_first, last_second)
+    z_parts, x_parts = (z_parts_a, z_parts_b, z_parts_c), (x_parts_a, x_parts_b, x_parts_c)
+    z_sums, x_sums = (z_sums_a, z_sums_b, z_sums_c), (x_sums_a, x_sums_b, x_sums_c)
+    last = ((z_last_a, x_last_a), (z_last_b, x_last_b), (z_last_c, x_last_c, y_last))
+    gram = (gram_a, gram_b, gram_c)
+    total, final = (total_a, total_b, total_c), (final_a, final_b, final_c)
     j = lax.axis_index("subj")
     v = lax.axis_index("vox")
     near, far, core = j ^ 1, j ^ 2, j & 1
@@ -299,20 +324,49 @@
             s = p // EP
             line = line_of(slot_of(j, taker), p - s * EP, s)
 
-            def put(first, rows, lines):
-                put_columns[i, pl.ds(first, rows), :] = jnp.where(lines == to, 1.0, 0.0).astype(BF16)
-
-            across = lax.broadcasted_iota(I32, (1, 128), 1)
-            down = lax.broadcasted_iota(I32, (128, 1), 0)
-            for n in range(2):
-                put(n * 320, 128, down)
-                put(n * 320 + 128, 128, (down & 63) + (n + 1) * 64)
-                put(n * 320 + 256, 64, lax.broadcasted_iota(I32, (64, 1), 0) + n * 128)
-                rows = lax.broadcasted_iota(I32, (1, 64), 1)
-                pick_rows[i, 2 * n] = jnp.where(rows + n * 128 == line, 1.0, 0.0).astype(BF16)
-                pick_rows[i, 2 * n + 1] = jnp.where(rows + (n + 1) * 64 == line, 1.0, 0.0).astype(BF16)
-                turned = across if n else jnp.where(across < 64, -1, across)
-                pick_turned[i, n] = jnp.where(turned == line, 1.0, 0.0).astype(BF16)
+            def put(first, lines):
+                put_columns[i, pl.ds(first, lines.shape[0]), :] = jnp.where(lines == to, 1.0, 0.0).astype(BF16)
+
+            def hot(lines):
+                return jnp.where(lines == line, 1.0, 0.0).astype(BF16)
+
+            def down(count):
+                return lax.broadcasted_iota(I32, (count, 1), 0)
+
+            def across(count):
+                return lax.broadcasted_iota(I32, (1, count), 1)
+
+            c, r = down(128), down(64)
+            around = (c & 63) + 64
+            put(0, jnp.where(c < 64, c, c - 32))
+            put(128, jnp.where(around < 96, around, around - 96))
+            put(256, jnp.where(r < 32, r, jnp.where(r < 48, r + 32, -1)))
+            put(320, jnp.where(r < 48, jnp.where(r < 32, r + 32, r + 48), -1))
+            c, r = across(128), across(64)
+            around = (c & 63) + 64
+            apart = (c & 32) > 0
+            for piece, (lines, columns) in enumerate(
+                (
+                    (jnp.where(r < 32, r, -1), jnp.where(apart & (c < 64), c, -1)),
+                    (jnp.where(r < 32, r + 32, -1), jnp.where(apart & (c >= 64), c - 32, -1)),
+                    (jnp.where((r >= 32) & (r < 48), r + 32, -1), jnp.where(apart & (c < 64), around - 96, -1)),
+                    (jnp.where((r >= 32) & (r < 48), r + 48, -1), jnp.where(apart & (c >= 64), around - 96, -1)),
+                )
+            ):
+                pick_a[i, pl.ds(piece * 48, 48), :] = hot(lines)
+                turn_a[i, pl.ds(piece * 48, 48), :] = hot(columns)
+            put(384, down(128))
+            put(512, down(32) + 96)
+            pick_b[i] = hot(across(32) + 96)
+            turn_b[i] = hot(jnp.where(c < 96, c, -1))
+            put(544, down(128))
+            put(672, (down(128) & 63) + 128)
+            put(800, down(64) + 128)
+            pick_wide[i] = hot(r + 128)
+            pick_square[i] = hot(r + 128)
+            turn_c[i] = hot(c)
+        for k in range(OWN):
+            score[k, 96:128, :] = jnp.zeros((32, VOX), BF16)
 
     for h in range(2):
         scales(1, h)
@@ -382,16 +436,28 @@
                 at = r * 48 + q * 16
                 score[k, pl.ds(at, 16), lanes] = both
 
-    split = ((48, 48, 0), (32, 32, 32))
+    split = ((32, 16, 0), (16, 16, 0), (32, 32, 32))
+    lane = lax.broadcasted_iota(I32, (16, 128), 1)
+
+    def against(m, first, count, columns=slice(0, 128)):
+        return lax.dot_general(score[m, pl.ds(first, count), :], score[m, columns, :], NT, preferred_element_type=F32)
 
     def block_of(n, m):
-        top = pl.ds(n * 128, 64)
-        gram[n, m, 0:64, :] = lax.dot_general(
-            score[m, top, :], score[m, pl.ds(0, 128), :], NT, preferred_element_type=F32
-        )
-        rows = score[m, pl.ds((n + 1) * 64, 64), :]
-        square = lax.dot_general(rows, rows, NT, preferred_element_type=F32)
-        gram[n, m, 64:96, :] = jnp.concatenate([square[0:32], square[32:64]], axis=1)
+        if n == 0:
+            block = against(m, 0, 96)
+            for top in (0, 16):
+                beside = pltpu.roll(block[32 + top : 48 + top], 32, 1)
+                gram[n][m, top : top + 16, :] = jnp.where(lane < 64, block[top : top + 16], beside)
+            upper, lower = block[64:80], block[80:96]
+            left = jnp.where(lane < 32, pltpu.roll(upper, 64, 1), pltpu.roll(upper, 32, 1))
+            right = jnp.where(lane < 96, lower, pltpu.roll(lower, 96, 1))
+            gram[n][m, 32:48, :] = jnp.where(lane < 64, left, right)
+        elif n == 1:
+            gram[n][m] = against(m, 96, 32)
+        else:
+            gram[n][m, 0:64, :] = against(m, 128, 64)
+            square = against(m, 128, 64, slice(128, 192))
+            gram[n][m, 64:96, :] = jnp.concatenate([square[0:32], square[32:64]], axis=1)
 
     def kernels(n, unfinished=None):
         z_rows, x_rows, y_rows = split[n]
@@ -411,20 +477,20 @@
 
                 @pl.when(major > 0)
                 def _():
-                    source = gram.at[n, m, pl.ds(0, z_rows)]
+                    source = gram[n].at[m, pl.ds(0, z_rows)]
                     to_v = shard_at(ahead_of(z, major), x, y)
                     copy_to(source, z_parts[n].at[minor, major], part_send.at[n], z_recv.at[n, minor], j, to_v).start()
 
                 @pl.when(minor > 0)
                 def _():
-                    source = gram.at[n, m, pl.ds(z_rows, x_rows)]
+                    source = gram[n].at[m, pl.ds(z_rows, x_rows)]
                     to_v = shard_at(z, ahead_of(x, minor), y)
                     copy_to(source, x_parts[n].at[major, minor], part_send.at[n], x_recv.at[n, major], j, to_v).start()
 
                 if y_rows:
                     rows = pl.ds(pl.multiple_of(z_rows + x_rows + y_rows // 2 * (y ^ 1), 8), y_rows // 2)
                     copy_to(
-                        gram.at[n, m, rows], y_parts.at[step], part_send.at[n], y_recv.at[major], j, v ^ 1
+                        gram[n].at[m, rows], y_parts.at[step], part_send.at[n], y_recv.at[major], j, v ^ 1
                     ).start()
             return carry
 
@@ -441,7 +507,7 @@
             with jax.named_scope("part_wait"):
                 await_bytes(parts[n].at[step, pl.ds(1, 3)], recv.at[n, step])
             own = (ahead_of(z, step) * 4 + x) if block else (z * 4 + ahead_of(x, step))
-            own = gram[n, own, pl.ds(z_rows, x_rows) if block else pl.ds(0, z_rows), :]
+            own = gram[n][own, pl.ds(z_rows, x_rows) if block else pl.ds(0, z_rows), :]
             sums[n][step] = (own + parts[n][step, 1]) + (parts[n][step, 2] + parts[n][step, 3])
             for other in range(2):
                 side = y ^ other
@@ -451,10 +517,10 @@
                 to_v = shard_at(ahead_of(z, step), x, side) if block else shard_at(z, ahead_of(x, step), side)
                 if slot:
                     copy_to(
-                        sums[n].at[step, rows], last[n].at[block * 8 + slot], sum_send.at[n], sum_recv.at[n], j, to_v
+                        sums[n].at[step, rows], last[n][block].at[slot], sum_send.at[n], sum_recv.at[n, block], j, to_v
                     ).start()
                 else:
-                    last[n][block * 8] = sums[n][0, rows, :]
+                    last[n][block][0] = sums[n][0, rows, :]
 
         def from_side(major):
             with jax.named_scope("part_wait"):
@@ -463,14 +529,14 @@
                 step = major * 4 + minor
                 to_z, to_x = ahead_of(z, major), ahead_of(x, minor)
                 rows = pl.ds(pl.multiple_of(z_rows + x_rows + y_rows // 2 * y, 8), y_rows // 2)
-                added = y_parts[step] + gram[n, to_z * 4 + to_x, rows, :]
+                added = y_parts[step] + gram[n][to_z * 4 + to_x, rows, :]
                 if step:
                     y_sums[step] = added
                     copy_to(
-                        y_sums.at[step], last[n].at[16 + step], sum_send.at[n], sum_recv.at[n], j, shard_at(to_z, to_x, y)
+                        y_sums.at[step], y_last.at[step], sum_send.at[n], sum_recv.at[n, 2], j, shard_at(to_z, to_x, y)
                     ).start()
                 else:
-                    last[n][16] = added
+                    y_last[0] = added
 
         if y_rows:
             for major in range(4):
@@ -486,21 +552,20 @@
 
     owner_v = v - y + j // 2
     place = core * 2 + y
-    remote_sums = (14, 29)
 
     def hand_over(n):
         with jax.named_scope("last_wait"):
-            await_bytes(last[n].at[pl.ds(0, remote_sums[n])], sum_recv.at[n])
+            for block, ref in enumerate(last[n]):
+                await_bytes(ref.at[pl.ds(0, ref.shape[0] - 1)], sum_recv.at[n, block])
         mean = 1.0 / (VOX * SHARDS)
         first = 0
-        for block, rows in enumerate(split[n]):
-            if rows:
-                slots = last[n][block * 8 : (block + (2 if block == 2 else 1)) * 8]
-                total[n, pl.ds(first, rows // 2), :] = jnp.sum(slots, axis=0) * mean
-                first += rows // 2
+        for ref in last[n]:
+            rows = ref.shape[1]
+            total[n][pl.ds(first, rows), :] = jnp.sum(ref[...], axis=0) * mean
+            first += rows
         for other in range(SUBJ):
             copy = copy_to(
-                total.at[n], final.at[n, place], final_send.at[n], final_recv.at[n], (j ^ other) if other else j, owner_v
+                total[n], final[n].at[place], final_send.at[n], final_recv.at[n], (j ^ other) if other else j, owner_v
             )
             if other:
                 copy.start()
@@ -512,16 +577,16 @@
 
         @pl.when(owner_v == v)
         def _():
-            final[n, place] = total[n]
+            final[n][place] = total[n][...]
 
     def await_final(n, sem):
         @pl.when(owner_v == v)
         def _():
-            await_bytes(final.at[n, pl.ds(0, SUBJ - 1)], sem.at[n])
+            await_bytes(final[n].at[pl.ds(0, SUBJ - 1)], sem.at[n])
 
         @pl.when(owner_v != v)
         def _():
-            await_bytes(final.at[n], sem.at[n])
+            await_bytes(final[n], sem.at[n])
 
     def scores_of(correlated, finished):
         with jax.named_scope("scores"):
@@ -542,58 +607,79 @@
     relayed(0)
     scores_of(4, 3)
     relay(1, 0)
+    kernels(0)
     scores_of(5, 4)
-    scores_of(None, 5)
+    kernels(1, 5)
     relay(1, 1)
-    kernels(0)
+    second_sums(0)
     relay(1, 2)
     relayed(1)
     scores_of(6, None)
     scores_of(7, 6)
-    kernels(1, 7)
-    second_sums(0)
+    kernels(2, 7)
     second_sums(1)
     hand_over(0)
+    second_sums(2)
     hand_over(1)
 
-    beside = lax.broadcasted_iota(I32, (EP * LOCAL, 128), 1) < 64
+    straight = (((1,), (0,)), ((), ()))
+    left = lax.broadcasted_iota(I32, (EP * LOCAL, 128), 1) < 64
+    upper = lax.broadcasted_iota(I32, (EP * LOCAL, 64), 1) < 32
+    puts = (0, 384, 544, 864)
 
     def picked_by(pick, terms, dims):
         parts = [lax.dot_general(pick, t, dims, preferred_element_type=F32) for t in terms]
-        return parts[0] + parts[1] + parts[2]
+        return parts[0] + parts[1]
 
     def placed(n, i):
         pieces, first = [], 0
         for rows in split[n]:
             if rows:
                 here = pl.ds(first, rows // 2)
-                pieces += [final[n, 2 * i, here, :], final[n, 2 * i + 1, here, :]]
+                pieces += [final[n][2 * i, here, :], final[n][2 * i + 1, here, :]]
                 first += rows // 2
-        both = jnp.concatenate(pieces, axis=0)
-        wide, square = exact_terms(both[0:64]), exact_terms(both[64:96])
-        halves = [
-            picked_by(pick_rows[i, 2 * n + 1, :, h * 32 : h * 32 + 32], square, (((1,), (0,)), ((), ())))
-            for h in range(2)
-        ]
-        lines = [
-            picked_by(pick_rows[i, 2 * n], wide, (((1,), (0,)), ((), ()))),
-            jnp.where(beside, halves[0], halves[1]),
-            picked_by(pick_turned[i, n], wide, NT),
-        ]
-        put = put_columns[i, pl.ds(n * 320, 320), :]
-        terms = [jnp.dot(t, put, preferred_element_type=F32) for t in exact_terms(jnp.concatenate(lines, axis=1))]
-        return terms[0] + terms[1] + terms[2]
+        if n == 0:
+            terms = two_terms(jnp.concatenate(pieces + [jnp.zeros((16, 128), F32)], axis=0))
+            by_row = picked_by(pick_a[i], terms, straight)
+            by_column = picked_by(turn_a[i], terms, NT)
+            lines = [
+                jnp.where(left, by_row[0:48], by_row[48:96]),
+                jnp.where(left, by_row[96:144], by_row[144:192]),
+                jnp.where(upper, by_column[0:48], by_column[96:144]),
+                jnp.where(upper, by_column[48:96], by_column[144:192]),
+            ]
+        elif n == 1:
+            terms = two_terms(jnp.concatenate(pieces, axis=0))
+            lines = [picked_by(pick_b[i], terms, straight), picked_by(turn_b[i], terms, NT)]
+        else:
+            both = jnp.concatenate(pieces, axis=0)
+            wide, square = two_terms(both[0:64]), two_terms(both[64:96])
+            halves = [picked_by(pick_square[i, :, h * 32 : h * 32 + 32], square, straight) for h in range(2)]
+            lines = [
+                picked_by(pick_wide[i], wide, straight),
+                jnp.where(left, halves[0], halves[1]),
+                picked_by(turn_c[i], wide, NT),
+            ]
+        put = put_columns[i, puts[n] : puts[n + 1], :]
+        terms = [jnp.dot(t, put, preferred_element_type=F32) for t in two_terms(jnp.concatenate(lines, axis=1))]
+        return terms[0] + terms[1]
 
     with jax.named_scope("final"):
         await_final(0, final_recv)
     with jax.named_scope("place"):
         for i in range(2):
             out_ref[i] = placed(0, i)
+    hand_over(2)
     with jax.named_scope("final"):
         await_final(1, final_recv)
     with jax.named_scope("place"):
         for i in range(2):
             out_ref[i] += placed(1, i)
+    with jax.named_scope("final"):
+        await_final(2, final_recv)
+    with jax.named_scope("place"):
+        for i in range(2):
+            out_ref[i] += placed(2, i)
 
     with jax.named_scope("drain"):
         await_bytes(slab_in.at[pl.ds(0, SHARDS - 1)], share_send)
@@ -606,12 +692,13 @@
         def _():
             await_bytes(slab_in, slab_send)
 
-        for n in range(2):
+        for n in range(3):
             await_bytes(z_parts[n].at[pl.ds(0, 3)], part_send.at[n])
             await_bytes(x_parts[n].at[pl.ds(0, 3)], part_send.at[n])
-            await_bytes(last[n].at[pl.ds(0, remote_sums[n])], sum_send.at[n])
+            for ref in last[n]:
+                await_bytes(ref.at[pl.ds(0, ref.shape[0] - 1)], sum_send.at[n])
             await_final(n, final_send)
-        await_bytes(y_parts, part_send.at[1])
+        await_bytes(y_parts, part_send.at[2])
         for q in range(QUADS):
             near_copy(q).wait_send()
             for h in range(2):
@@ -650,24 +737,44 @@
             vmem((QUADS, 256, 256), F32),
             vmem((QUADS, 256, 256), F32),
             vmem((OWN, ROWS, VOX), BF16),
-            vmem((2, OWN, 96, 128), F32),
-            vmem((4, 4, 48, 128), F32),
+            vmem((OWN, 48, 128), F32),
+            vmem((OWN, 32, 128), F32),
+            vmem((OWN, 96, 128), F32),
             vmem((4, 4, 32, 128), F32),
-            vmem((4, 4, 48, 128), F32),
+            vmem((4, 4, 16, 128), F32),
+            vmem((4, 4, 32, 128), F32),
+            vmem((4, 4, 16, 128), F32),
+            vmem((4, 4, 16, 128), F32),
             vmem((4, 4, 32, 128), F32),
             vmem((OWN, 16, 128), F32),
-            vmem((4, 48, 128), F32),
             vmem((4, 32, 128), F32),
-            vmem((4, 48, 128), F32),
+            vmem((4, 16, 128), F32),
+            vmem((4, 32, 128), F32),
+            vmem((4, 16, 128), F32),
+            vmem((4, 16, 128), F32),
             vmem((4, 32, 128), F32),
             vmem((OWN, 16, 128), F32),
-            vmem((16, 24, 128), F32),
-            vmem((32, 16, 128), F32),
-            vmem((2, 48, 128), F32),
-            vmem((2, SUBJ, 48, 128), F32),
-            vmem((2, 4, EP * LOCAL, 64), BF16),
-            vmem((2, 2, EP * LOCAL, 128), BF16),
-            vmem((2, 5 * 128, ROWS), BF16),
+            vmem((8, 16, 128), F32),
+            vmem((8, 8, 128), F32),
+            vmem((8, 16, 128), F32),
+            vmem((8, 8, 128), F32),
+            vmem((8, 8, 128), F32),
+            vmem((8, 16, 128), F32),
+            vmem((OWN, 16, 128), F32),
+            vmem((24, 128), F32),
+            vmem((16, 128), F32),
+            vmem((48, 128), F32),
+            vmem((SUBJ, 24, 128), F32),
+            vmem((SUBJ, 16, 128), F32),
+            vmem((SUBJ, 48, 128), F32),
+            vmem((2, 4 * EP * LOCAL, 64), BF16),
+            vmem((2, EP * LOCAL, 32), BF16),
+            vmem((2, EP * LOCAL, 64), BF16),
+            vmem((2, EP * LOCAL, 64), BF16),
+            vmem((2, 4 * EP * LOCAL, 128), BF16),
+            vmem((2, EP * LOCAL, 128), BF16),
+            vmem((2, EP * LOCAL, 128), BF16),
+            vmem((2, 864, ROWS), BF16),
             dma((3,)),
             dma,
             dma,
@@ -679,14 +786,14 @@
             dma((2 * QUADS,)),
             dma((2 * QUADS,)),
             dma((2 * QUADS,)),
-            dma((2,)),
-            dma((2, 4)),
-            dma((2, 4)),
+            dma((3,)),
+            dma((3, 4)),
+            dma((3, 4)),
             dma((4,)),
-            dma((2,)),
-            dma((2,)),
-            dma((2,)),
-            dma((2,)),
+            dma((3,)),
+            dma((3, 3)),
+            dma((3,)),
+            dma((3,)),
         ],
         compiler_params=pltpu.CompilerParams(collective_id=0, has_side_effects=True),
     )(series, offsets, selected)

time: 50.3 us -> 51.9 us (1.032)
  Pallas kernels: 49.5 us -> 51.2 us
    pallas_call x1, Pallas kernels: 49.5 us -> 51.2 us  [body(): pl.pallas_call(main_kernel, out_shape=pltpu.VMEM((2, EP * LOCAL, ROWS), F...]
where the time goes in v7:
time: 51.9 us; the launch traced here: 51.8 us
  Pallas kernels  51.2 us (99%)
  local copies, waits for them, and re-layouts  0.64 us (1%)
    pallas_call x1, Pallas kernels, body(): pl.pallas_call(main_kernel, out_shape=pltpu.VMEM((2, EP * LOCAL, ROWS), F...  51.2 us

profile of v7, /device:TPU:1, one launch (start us, length us, event | category | flops | bytes accessed | tf_op | source)
XLA Modules:
  0.0 51.8 jit_solution(7008414458920959842)
XLA Ops:
  0.0 51.2 %shard_map.37 = f32[2,48,192]{2,1,0:T(8,128)S(1)} custom-call(bf16[4,256,512]{2,1,0:T(8,128)(2,1)} %series_hbm.1, s32[16,12]{1,0:T(8,128)} %offsets_hbm.1, s32[64]{0:T(128)} %selected_hbm.1), custom_call_target="tpu_custom_call" | custom-call | tf_op jit(solution)/shard_map/pallas_call | solution.py:712
  51.2 0.6 %copy.5 = f32[2,48,192]{2,1,0:T(8,128)} copy(f32[2,48,192]{2,1,0:T(8,128)S(1)} %shard_map.37) | data formatting | bytes 147456

commit v8 on v7

--- a/solution.py
+++ b/solution.py
@@ -219,7 +219,8 @@
         runs = series[...].reshape(LOCAL * RUN, VOX)
         for q in range(QUADS):
             chosen = jnp.dot(choose[pl.ds(q * 256, 256), :], runs, preferred_element_type=F32).astype(BF16)
-            epochs[0, q] = chosen
+            for h in range(2):
+                epochs[0, h, q] = chosen[:, h * 256 : h * 256 + 256]
             picked = lax.dot_general(picker, chosen, NT, preferred_element_type=F32)
             slab_out[:, :, pl.ds(q * 256, 256)] = picked.astype(BF16).reshape(SHARDS, 2, 256)
 
@@ -239,19 +240,17 @@
     with jax.named_scope("send_slab"):
         lax.fori_loop(0, SHARDS, send_slab, 0)
 
-    def near_copy(q):
-        return copy_to(epochs.at[0, q], epochs.at[1, q], near_send.at[q], near_recv.at[q], near, v)
-
-    half = pl.ds(pl.multiple_of(core * 256, 256), 256)
+    def near_copy(h):
+        return copy_to(epochs.at[0, h], epochs.at[1, h], near_send.at[h], near_recv.at[h], near, v)
 
     def far_copy(g, q):
         at = g * QUADS + q
-        source, target = epochs.at[core ^ g, q, :, half], epochs.at[2 + g, q, :, half]
+        source, target = epochs.at[core ^ g, core, q], epochs.at[2 + g, core, q]
         return copy_to(source, target, far_send.at[at], far_recv.at[at], far, v)
 
     def relay_copy(g, q):
         at = g * QUADS + q
-        ref = epochs.at[2 + g, q, :, half]
+        ref = epochs.at[2 + g, core, q]
         return copy_to(ref, ref, relay_send.at[at], relay_recv.at[at], near, v)
 
     def relay(g, q):
@@ -259,17 +258,20 @@
             far_copy(g, q).wait_recv()
             relay_copy(g, q).start()
 
-    for q in range(QUADS):
-        near_copy(q).start()
+    for h in (1, 0):
+        near_copy(h).start()
 
     @pl.when(core == 0)
     def _():
         far_copy(0, 0).start()
 
+    def lanes_of(h):
+        return pl.ds(h * 256 if isinstance(h, int) else pl.multiple_of(h * 256, 256), 256)
+
     def scales(r, h):
-        lanes = pl.ds(h * 256, 256)
+        lanes = lanes_of(h)
         for q in range(QUADS):
-            seen = epochs[r, q, :, lanes].astype(F32).reshape(TR, 16, 256)
+            seen = epochs[r, h, q].astype(F32).reshape(TR, 16, 256)
             centred = seen - (jnp.sum(seen, axis=0) * (1.0 / TR))[None]
             scale[r, q, :, lanes] = lax.rsqrt(jnp.sum(centred * centred, axis=0) + series_floor)
 
@@ -277,8 +279,8 @@
         scales(0, h)
 
     with jax.named_scope("near_wait"):
-        for q in range(QUADS):
-            near_copy(q).wait_recv()
+        for h in range(2):
+            near_copy(h).wait_recv()
 
     @pl.when(core == 1)
     def _():
@@ -398,28 +400,28 @@
 
     own_row = (lax.broadcasted_iota(I32, (16, 256), 1) & 15) == lax.broadcasted_iota(I32, (16, 256), 0)
 
-    units = ((0, 0), (0, 1), (1, 0), (1, 1), (2, 0), (2, 1), (3, 0), (3, 1))
+    units = ((0, 0), (0, 1), (1, 0), (1, 1), (2, 0), (2, 1), (3, core), (3, 1 - core))
 
     def correlate(unit):
         r, h = units[unit]
-        lanes = pl.ds(h * 256, 256)
+        lanes = lanes_of(h)
         if r >= 2:
             scales(r, h)
         for q in range(QUADS):
             at = r * QUADS + q
-            if h == 0:
+            if unit % 2 == 0:
                 for k in range(OWN):
                     for std, lhs in ((std_hi, lhs_hi), (std_lo, lhs_lo)):
                         line = jnp.broadcast_to(std[at, pl.ds(k, 1), :], (16, 256))
                         lhs[at, pl.ds(k * 16, 16), :] = jnp.where(own_row, line, 0.0).astype(BF16)
-            seen = epochs[r, q, :, lanes]
+            seen = epochs[r, h, q]
             corr[unit % 2][q] = jnp.dot(lhs_hi[at], seen, preferred_element_type=F32) + jnp.dot(
                 lhs_lo[at], seen, preferred_element_type=F32
             )
 
     def standard(unit, ids=range(OWN)):
         r, h = units[unit]
-        lanes = pl.ds(h * 256, 256)
+        lanes = lanes_of(h)
         for k in ids:
             rows = pl.ds(k * 16 if isinstance(k, int) else pl.multiple_of(k * 16, 16), 16)
             halves = []
@@ -611,11 +613,12 @@
     scores_of(5, 4)
     kernels(1, 5)
     relay(1, 1)
+    relay(1, 2)
+    scores_of(6, None)
+    scores_of(None, 6)
     second_sums(0)
-    relay(1, 2)
     relayed(1)
-    scores_of(6, None)
-    scores_of(7, 6)
+    scores_of(7, None)
     kernels(2, 7)
     second_sums(1)
     hand_over(0)
@@ -699,9 +702,9 @@
                 await_bytes(ref.at[pl.ds(0, ref.shape[0] - 1)], sum_send.at[n])
             await_final(n, final_send)
         await_bytes(y_parts, part_send.at[2])
-        for q in range(QUADS):
-            near_copy(q).wait_send()
-            for h in range(2):
+        for h in range(2):
+            near_copy(h).wait_send()
+            for q in range(QUADS):
                 far_copy(h, q).wait_send()
                 relay_copy(h, q).wait_send()
 
@@ -723,7 +726,7 @@
             pltpu.SMEM((SEL,), I32),
             vmem((LOCAL, RUN, VOX), BF16),
             vmem((QUADS * 256, LOCAL * RUN), BF16),
-            vmem((SUBJ, QUADS, 256, VOX), BF16),
+            vmem((SUBJ, 2, QUADS, 256, 256), BF16),
             vmem((SUBJ, QUADS, 16, VOX), F32),
             vmem((SHARDS, 2, QUADS * 256), BF16),
             vmem((SHARDS, 2, QUADS * 256), BF16),
@@ -780,8 +783,8 @@
             dma,
             dma,
             dma,
-            dma((QUADS,)),
-            dma((QUADS,)),
+            dma((2,)),
+            dma((2,)),
             dma((2 * QUADS,)),
             dma((2 * QUADS,)),
             dma((2 * QUADS,)),

time: 51.9 us -> 50.9 us (0.981)
  Pallas kernels: 51.2 us -> 50.1 us
    pallas_call x1, Pallas kernels: 51.2 us -> 50.1 us  [body(): pl.pallas_call(main_kernel, out_shape=pltpu.VMEM((2, EP * LOCAL, ROWS), F...]
where the time goes in v8:
time: 50.9 us; the launch traced here: 50.8 us
  Pallas kernels  50.1 us (98%)
  local copies, waits for them, and re-layouts  0.64 us (1%)
    pallas_call x1, Pallas kernels, body(): pl.pallas_call(main_kernel, out_shape=pltpu.VMEM((2, EP * LOCAL, ROWS), F...  50.1 us

profile of v8, /device:TPU:1, one launch (start us, length us, event | category | flops | bytes accessed | tf_op | source)
XLA Modules:
  0.0 50.8 jit_solution(1384410085161326262)
XLA Ops:
  0.0 50.1 %shard_map.37 = f32[2,48,192]{2,1,0:T(8,128)S(1)} custom-call(bf16[4,256,512]{2,1,0:T(8,128)(2,1)} %series_hbm.1, s32[16,12]{1,0:T(8,128)} %offsets_hbm.1, s32[64]{0:T(128)} %selected_hbm.1), custom_call_target="tpu_custom_call" | custom-call | tf_op jit(solution)/shard_map/pallas_call | solution.py:715
  50.1 0.6 %copy.5 = f32[2,48,192]{2,1,0:T(8,128)} copy(f32[2,48,192]{2,1,0:T(8,128)S(1)} %shard_map.37) | data formatting | bytes 147456

commit v9 on v8

--- a/solution.py
+++ b/solution.py
@@ -217,8 +217,9 @@
     with jax.named_scope("pick_epochs"):
         loads[2].wait()
         runs = series[...].reshape(LOCAL * RUN, VOX)
+        all_chosen = jnp.dot(choose[...], runs, preferred_element_type=F32).astype(BF16)
         for q in range(QUADS):
-            chosen = jnp.dot(choose[pl.ds(q * 256, 256), :], runs, preferred_element_type=F32).astype(BF16)
+            chosen = all_chosen[q * 256 : q * 256 + 256]
             for h in range(2):
                 epochs[0, h, q] = chosen[:, h * 256 : h * 256 + 256]
             picked = lax.dot_general(picker, chosen, NT, preferred_element_type=F32)
@@ -464,8 +465,13 @@
     def kernels(n, unfinished=None):
         z_rows, x_rows, y_rows = split[n]
 
+        def offsets_at(step):
+            slow, fast = (step // 4 + 1) & 3, (step + 1) & 3
+            return slow ^ (slow >> 1), fast ^ (fast >> 1)
+
         def id_at(step):
-            return ahead_of(z, step // 4) * 4 + ahead_of(x, step & 3)
+            major, minor = offsets_at(step)
+            return ahead_of(z, major) * 4 + ahead_of(x, minor)
 
         def four(index, carry):
             steps = [index * 4 + more for more in range(8)]
@@ -474,7 +480,7 @@
             if unfinished is not None:
                 standard(unfinished, [id_at(step & 15) for step in steps[4:]])
             for step in steps[:4]:
-                major, minor = step // 4, step & 3
+                major, minor = offsets_at(step)
                 m = ahead_of(z, major) * 4 + ahead_of(x, minor)
 
                 @pl.when(major > 0)
@@ -492,7 +498,7 @@
                 if y_rows:
                     rows = pl.ds(pl.multiple_of(z_rows + x_rows + y_rows // 2 * (y ^ 1), 8), y_rows // 2)
                     copy_to(
-                        gram[n].at[m, rows], y_parts.at[step], part_send.at[n], y_recv.at[major], j, v ^ 1
+                        gram[n].at[m, rows], y_parts.at[major * 4 + minor], part_send.at[n], y_recv.at[major], j, v ^ 1
                     ).start()
             return carry
 
@@ -541,16 +547,14 @@
                     y_last[0] = added
 
         if y_rows:
-            for major in range(4):
+            for major in (1, 3, 2, 0):
                 along(major, 1)
                 from_side(major)
-            for step in range(4):
-                along(step, 0)
         else:
-            for step in range(4):
+            for step in (1, 3, 2, 0):
                 along(step, 1)
-            for step in range(4):
-                along(step, 0)
+        for step in (1, 3, 2, 0):
+            along(step, 0)
 
     owner_v = v - y + j // 2
     place = core * 2 + y
@@ -621,8 +625,8 @@
     scores_of(7, None)
     kernels(2, 7)
     second_sums(1)
+    second_sums(2)
     hand_over(0)
-    second_sums(2)
     hand_over(1)
 
     straight = (((1,), (0,)), ((), ()))

time: 50.9 us -> 50.2 us (0.986)
  Pallas kernels: 50.1 us -> 49.4 us
    pallas_call x1, Pallas kernels: 50.1 us -> 49.4 us  [body(): pl.pallas_call(main_kernel, out_shape=pltpu.VMEM((2, EP * LOCAL, ROWS), F...]
where the time goes in v9:
time: 50.2 us; the launch traced here: 50.1 us
  Pallas kernels  49.4 us (98%)
  local copies, waits for them, and re-layouts  0.64 us (1%)
    pallas_call x1, Pallas kernels, body(): pl.pallas_call(main_kernel, out_shape=pltpu.VMEM((2, EP * LOCAL, ROWS), F...  49.4 us

profile of v9, /device:TPU:1, one launch (start us, length us, event | category | flops | bytes accessed | tf_op | source)
XLA Modules:
  0.0 50.1 jit_solution(15412233819339762559)
XLA Ops:
  0.0 49.4 %shard_map.37 = f32[2,48,192]{2,1,0:T(8,128)S(1)} custom-call(bf16[4,256,512]{2,1,0:T(8,128)(2,1)} %series_hbm.1, s32[16,12]{1,0:T(8,128)} %offsets_hbm.1, s32[64]{0:T(128)} %selected_hbm.1), custom_call_target="tpu_custom_call" | custom-call | tf_op jit(solution)/shard_map/pallas_call | solution.py:719
  49.4 0.6 %copy.5 = f32[2,48,192]{2,1,0:T(8,128)} copy(f32[2,48,192]{2,1,0:T(8,128)S(1)} %shard_map.37) | data formatting | bytes 147456

commit v10 on v9

--- a/solution.py
+++ b/solution.py
@@ -359,13 +359,14 @@
                 pick_a[i, pl.ds(piece * 48, 48), :] = hot(lines)
                 turn_a[i, pl.ds(piece * 48, 48), :] = hot(columns)
             put(384, down(128))
-            put(512, down(32) + 96)
-            pick_b[i] = hot(across(32) + 96)
-            turn_b[i] = hot(jnp.where(c < 96, c, -1))
-            put(544, down(128))
-            put(672, (down(128) & 63) + 128)
-            put(800, down(64) + 128)
-            pick_wide[i] = hot(r + 128)
+            put(512, down(48) + 96)
+            pick_b[i] = hot(across(48) + 96)
+            turn_b[i, 0:48, :] = hot(jnp.where(c < 96, c, -1))
+            turn_b[i, 48:96, :] = hot(jnp.where(c < 96, -1, c))
+            put(560, down(128))
+            put(688, (down(128) & 63) + 128)
+            put(816, down(48) + 144)
+            pick_wide[i] = hot(across(48) + 144)
             pick_square[i] = hot(r + 128)
             turn_c[i] = hot(c)
         for k in range(OWN):
@@ -439,7 +440,7 @@
                 at = r * 48 + q * 16
                 score[k, pl.ds(at, 16), lanes] = both
 
-    split = ((32, 16, 0), (16, 16, 0), (32, 32, 32))
+    split = ((32, 16, 0), (16, 32, 0), (32, 32, 16))
     lane = lax.broadcasted_iota(I32, (16, 128), 1)
 
     def against(m, first, count, columns=slice(0, 128)):
@@ -456,11 +457,11 @@
             right = jnp.where(lane < 96, lower, pltpu.roll(lower, 96, 1))
             gram[n][m, 32:48, :] = jnp.where(lane < 64, left, right)
         elif n == 1:
-            gram[n][m] = against(m, 96, 32)
+            gram[n][m] = against(m, 96, 48)
         else:
-            gram[n][m, 0:64, :] = against(m, 128, 64)
+            gram[n][m, 0:48, :] = against(m, 144, 48)
             square = against(m, 128, 64, slice(128, 192))
-            gram[n][m, 64:96, :] = jnp.concatenate([square[0:32], square[32:64]], axis=1)
+            gram[n][m, 48:80, :] = jnp.concatenate([square[0:32], square[32:64]], axis=1)
 
     def kernels(n, unfinished=None):
         z_rows, x_rows, y_rows = split[n]
@@ -632,7 +633,8 @@
     straight = (((1,), (0,)), ((), ()))
     left = lax.broadcasted_iota(I32, (EP * LOCAL, 128), 1) < 64
     upper = lax.broadcasted_iota(I32, (EP * LOCAL, 64), 1) < 32
-    puts = (0, 384, 544, 864)
+    puts = (0, 384, 560, 864)
+    corner = lax.broadcasted_iota(I32, (EP * LOCAL, 48), 1) >= 32
 
     def picked_by(pick, terms, dims):
         parts = [lax.dot_general(pick, t, dims, preferred_element_type=F32) for t in terms]
@@ -657,10 +659,12 @@
             ]
         elif n == 1:
             terms = two_terms(jnp.concatenate(pieces, axis=0))
-            lines = [picked_by(pick_b[i], terms, straight), picked_by(turn_b[i], terms, NT)]
+            by_column = picked_by(turn_b[i], terms, NT)
+            turned = by_column[0:48] + jnp.where(corner, by_column[48:96], 0.0)
+            lines = [picked_by(pick_b[i], terms, straight), turned]
         else:
             both = jnp.concatenate(pieces, axis=0)
-            wide, square = two_terms(both[0:64]), two_terms(both[64:96])
+            wide, square = two_terms(both[0:48]), two_terms(both[48:80])
             halves = [picked_by(pick_square[i, :, h * 32 : h * 32 + 32], square, straight) for h in range(2)]
             lines = [
                 picked_by(pick_wide[i], wide, straight),
@@ -745,41 +749,41 @@
             vmem((QUADS, 256, 256), F32),
             vmem((OWN, ROWS, VOX), BF16),
             vmem((OWN, 48, 128), F32),
-            vmem((OWN, 32, 128), F32),
-            vmem((OWN, 96, 128), F32),
+            vmem((OWN, 48, 128), F32),
+            vmem((OWN, 80, 128), F32),
             vmem((4, 4, 32, 128), F32),
             vmem((4, 4, 16, 128), F32),
             vmem((4, 4, 32, 128), F32),
             vmem((4, 4, 16, 128), F32),
-            vmem((4, 4, 16, 128), F32),
             vmem((4, 4, 32, 128), F32),
-            vmem((OWN, 16, 128), F32),
+            vmem((4, 4, 32, 128), F32),
+            vmem((OWN, 8, 128), F32),
             vmem((4, 32, 128), F32),
             vmem((4, 16, 128), F32),
             vmem((4, 32, 128), F32),
             vmem((4, 16, 128), F32),
-            vmem((4, 16, 128), F32),
             vmem((4, 32, 128), F32),
-            vmem((OWN, 16, 128), F32),
+            vmem((4, 32, 128), F32),
+            vmem((OWN, 8, 128), F32),
             vmem((8, 16, 128), F32),
             vmem((8, 8, 128), F32),
             vmem((8, 16, 128), F32),
             vmem((8, 8, 128), F32),
-            vmem((8, 8, 128), F32),
             vmem((8, 16, 128), F32),
-            vmem((OWN, 16, 128), F32),
+            vmem((8, 16, 128), F32),
+            vmem((OWN, 8, 128), F32),
             vmem((24, 128), F32),
-            vmem((16, 128), F32),
-            vmem((48, 128), F32),
+            vmem((24, 128), F32),
+            vmem((40, 128), F32),
             vmem((SUBJ, 24, 128), F32),
-            vmem((SUBJ, 16, 128), F32),
-            vmem((SUBJ, 48, 128), F32),
+            vmem((SUBJ, 24, 128), F32),
+            vmem((SUBJ, 40, 128), F32),
             vmem((2, 4 * EP * LOCAL, 64), BF16),
-            vmem((2, EP * LOCAL, 32), BF16),
-            vmem((2, EP * LOCAL, 64), BF16),
+            vmem((2, EP * LOCAL, 48), BF16),
+            vmem((2, EP * LOCAL, 48), BF16),
             vmem((2, EP * LOCAL, 64), BF16),
             vmem((2, 4 * EP * LOCAL, 128), BF16),
-            vmem((2, EP * LOCAL, 128), BF16),
+            vmem((2, 2 * EP * LOCAL, 128), BF16),
             vmem((2, EP * LOCAL, 128), BF16),
             vmem((2, 864, ROWS), BF16),
             dma((3,)),

time: 50.2 us -> 49.9 us (level)
  no operation moved by 1% of the time
where the time goes in v10:
time: 49.9 us; the launch traced here: 49.8 us
  Pallas kernels  49.2 us (99%)
  local copies, waits for them, and re-layouts  0.64 us (1%)
    pallas_call x1, Pallas kernels, body(): pl.pallas_call(main_kernel, out_shape=pltpu.VMEM((2, EP * LOCAL, ROWS), F...  49.2 us

profile of v10, /device:TPU:1, one launch (start us, length us, event | category | flops | bytes accessed | tf_op | source)
XLA Modules:
  0.0 49.8 jit_solution(5237600037862900556)
XLA Ops:
  0.0 49.2 %shard_map.37 = f32[2,48,192]{2,1,0:T(8,128)S(1)} custom-call(bf16[4,256,512]{2,1,0:T(8,128)(2,1)} %series_hbm.1, s32[16,12]{1,0:T(8,128)} %offsets_hbm.1, s32[64]{0:T(128)} %selected_hbm.1), custom_call_target="tpu_custom_call" | custom-call | tf_op jit(solution)/shard_map/pallas_call | solution.py:723
  49.2 0.6 %copy.5 = f32[2,48,192]{2,1,0:T(8,128)} copy(f32[2,48,192]{2,1,0:T(8,128)S(1)} %shard_map.37) | data formatting | bytes 147456

commit v11 on v10

--- a/solution.py
+++ b/solution.py
@@ -183,7 +183,8 @@
         return carry
 
     with jax.named_scope("greet"):
-        lax.fori_loop(1, SHARDS, greet, 0, unroll=4)
+        lax.fori_loop(12, SHARDS, greet, 0, unroll=4)
+        lax.fori_loop(1, 12, greet, 0, unroll=11)
         for other in range(1, SUBJ):
             pl.semaphore_signal(barrier, inc=1, device_id={"subj": j ^ other, "vox": v}, device_id_type=MESH)
 
@@ -621,14 +622,15 @@
     relay(1, 2)
     scores_of(6, None)
     scores_of(None, 6)
-    second_sums(0)
     relayed(1)
     scores_of(7, None)
     kernels(2, 7)
+    second_sums(0)
     second_sums(1)
     second_sums(2)
     hand_over(0)
     hand_over(1)
+    hand_over(2)
 
     straight = (((1,), (0,)), ((), ()))
     left = lax.broadcasted_iota(I32, (EP * LOCAL, 128), 1) < 64
@@ -680,7 +682,6 @@
     with jax.named_scope("place"):
         for i in range(2):
             out_ref[i] = placed(0, i)
-    hand_over(2)
     with jax.named_scope("final"):
         await_final(1, final_recv)
     with jax.named_scope("place"):

time: 49.9 us -> 50.6 us (1.014)
  Pallas kernels: 49.2 us -> 49.8 us
    pallas_call x1, Pallas kernels: 49.2 us -> 49.8 us  [body(): pl.pallas_call(main_kernel, out_shape=pltpu.VMEM((2, EP * LOCAL, ROWS), F...]
where the time goes in v11:
time: 50.6 us; the launch traced here: 50.5 us
  Pallas kernels  49.8 us (98%)
  local copies, waits for them, and re-layouts  0.64 us (1%)
    pallas_call x1, Pallas kernels, body(): pl.pallas_call(main_kernel, out_shape=pltpu.VMEM((2, EP * LOCAL, ROWS), F...  49.8 us

profile of v11, /device:TPU:1, one launch (start us, length us, event | category | flops | bytes accessed | tf_op | source)
XLA Modules:
  0.0 50.5 jit_solution(16057191535420047124)
XLA Ops:
  0.0 49.8 %shard_map.37 = f32[2,48,192]{2,1,0:T(8,128)S(1)} custom-call(bf16[4,256,512]{2,1,0:T(8,128)(2,1)} %series_hbm.1, s32[16,12]{1,0:T(8,128)} %offsets_hbm.1, s32[64]{0:T(128)} %selected_hbm.1), custom_call_target="tpu_custom_call" | custom-call | tf_op jit(solution)/shard_map/pallas_call | solution.py:724
  49.8 0.6 %copy.5 = f32[2,48,192]{2,1,0:T(8,128)} copy(f32[2,48,192]{2,1,0:T(8,128)S(1)} %shard_map.37) | data formatting | bytes 147456

commit v12 on v11

--- a/solution.py
+++ b/solution.py
@@ -129,6 +129,8 @@
     slab_recv,
     share_send,
     share_recv,
+    partner_send,
+    partner_recv,
     near_send,
     near_recv,
     far_send,
@@ -183,8 +185,8 @@
         return carry
 
     with jax.named_scope("greet"):
-        lax.fori_loop(12, SHARDS, greet, 0, unroll=4)
-        lax.fori_loop(1, 12, greet, 0, unroll=11)
+        for step in range(1, SHARDS):
+            greet(step, 0)
         for other in range(1, SUBJ):
             pl.semaphore_signal(barrier, inc=1, device_id={"subj": j ^ other, "vox": v}, device_id_type=MESH)
 
@@ -306,13 +308,19 @@
     with jax.named_scope("slab_sum"):
         slab_sum[...] = jnp.sum(slab_in[...].astype(F32), axis=0).astype(BF16)
 
-    def share_slab(step, carry):
-        copy_to(slab_sum, slab.at[v], share_send, share_recv, j, (v + step) & (SHARDS - 1)).start()
-        return carry
-
-    with jax.named_scope("share_slab"):
-        lax.fori_loop(1, SHARDS, share_slab, 0)
-        slab[v] = slab_sum[...]
+    partner = copy_to(slab_sum, slab.at[v], partner_send, partner_recv, j, v ^ 1)
+
+    def share_slab(source, slot):
+        def send(step, carry):
+            copy_to(source, slab.at[slot], share_send, share_recv, j, (v + 2 * step) & (SHARDS - 1)).start()
+            return carry
+
+        with jax.named_scope("share_slab"):
+            lax.fori_loop(1, SHARDS // 2, send, 0)
+
+    partner.start()
+    share_slab(slab_sum, v)
+    slab[v] = slab_sum[...]
 
     far_copy(0, 2).start()
     for q in range(QUADS):
@@ -376,10 +384,13 @@
     for h in range(2):
         scales(1, h)
 
+    with jax.named_scope("partner_wait"):
+        partner.wait_recv()
+    share_slab(slab.at[v ^ 1], v ^ 1)
     relay(0, 0)
     relay(0, 1)
     with jax.named_scope("share_wait"):
-        await_bytes(slab.at[pl.ds(0, SHARDS - 1)], share_recv)
+        await_bytes(slab.at[pl.ds(0, SHARDS - 2)], share_recv)
     relay(0, 2)
 
     with jax.named_scope("standard_slab"):
@@ -624,8 +635,8 @@
     scores_of(None, 6)
     relayed(1)
     scores_of(7, None)
+    second_sums(0)
     kernels(2, 7)
-    second_sums(0)
     second_sums(1)
     second_sums(2)
     hand_over(0)
@@ -694,7 +705,8 @@
             out_ref[i] += placed(2, i)
 
     with jax.named_scope("drain"):
-        await_bytes(slab_in.at[pl.ds(0, SHARDS - 1)], share_send)
+        await_bytes(slab_in.at[pl.ds(0, SHARDS - 2)], share_send)
+        partner.wait_send()
 
         @pl.when(own_group)
         def _():
@@ -792,6 +804,8 @@
             dma,
             dma,
             dma,
+            dma,
+            dma,
             dma((2,)),
             dma((2,)),
             dma((2 * QUADS,)),

time: 50.6 us -> 50.2 us (level)
  no operation moved by 1% of the time
where the time goes in v12:
time: 50.2 us; the launch traced here: 50.1 us
  Pallas kernels  49.4 us (98%)
  local copies, waits for them, and re-layouts  0.64 us (1%)
    pallas_call x1, Pallas kernels, body(): pl.pallas_call(main_kernel, out_shape=pltpu.VMEM((2, EP * LOCAL, ROWS), F...  49.4 us

profile of v12, /device:TPU:1, one launch (start us, length us, event | category | flops | bytes accessed | tf_op | source)
XLA Modules:
  0.0 50.1 jit_solution(6907966788807506745)
XLA Ops:
  0.0 49.4 %shard_map.37 = f32[2,48,192]{2,1,0:T(8,128)S(1)} custom-call(bf16[4,256,512]{2,1,0:T(8,128)(2,1)} %series_hbm.1, s32[16,12]{1,0:T(8,128)} %offsets_hbm.1, s32[64]{0:T(128)} %selected_hbm.1), custom_call_target="tpu_custom_call" | custom-call | tf_op jit(solution)/shard_map/pallas_call | solution.py:736
  49.4 0.6 %copy.5 = f32[2,48,192]{2,1,0:T(8,128)} copy(f32[2,48,192]{2,1,0:T(8,128)S(1)} %shard_map.37) | data formatting | bytes 147456

commit v13 on v10

--- a/solution.py
+++ b/solution.py
@@ -614,8 +614,8 @@
     relayed(0)
     scores_of(4, 3)
     relay(1, 0)
-    kernels(0)
-    scores_of(5, 4)
+    kernels(0, 4)
+    scores_of(5, None)
     kernels(1, 5)
     relay(1, 1)
     relay(1, 2)
@@ -629,6 +629,7 @@
     second_sums(2)
     hand_over(0)
     hand_over(1)
+    hand_over(2)
 
     straight = (((1,), (0,)), ((), ()))
     left = lax.broadcasted_iota(I32, (EP * LOCAL, 128), 1) < 64
@@ -680,7 +681,6 @@
     with jax.named_scope("place"):
         for i in range(2):
             out_ref[i] = placed(0, i)
-    hand_over(2)
     with jax.named_scope("final"):
         await_final(1, final_recv)
     with jax.named_scope("place"):

time: 49.9 us -> 50 us (level)
  no operation moved by 1% of the time
where the time goes in v13:
time: 50 us; the launch traced here: 49.9 us
  Pallas kernels  49.2 us (98%)
  local copies, waits for them, and re-layouts  0.64 us (1%)
    pallas_call x1, Pallas kernels, body(): pl.pallas_call(main_kernel, out_shape=pltpu.VMEM((2, EP * LOCAL, ROWS), F...  49.2 us

profile of v13, /device:TPU:1, one launch (start us, length us, event | category | flops | bytes accessed | tf_op | source)
XLA Modules:
  0.0 49.9 jit_solution(13463645144799260763)
XLA Ops:
  0.0 49.2 %shard_map.37 = f32[2,48,192]{2,1,0:T(8,128)S(1)} custom-call(bf16[4,256,512]{2,1,0:T(8,128)(2,1)} %series_hbm.1, s32[16,12]{1,0:T(8,128)} %offsets_hbm.1, s32[64]{0:T(128)} %selected_hbm.1), custom_call_target="tpu_custom_call" | custom-call | tf_op jit(solution)/shard_map/pallas_call | solution.py:723
  49.2 0.6 %copy.5 = f32[2,48,192]{2,1,0:T(8,128)} copy(f32[2,48,192]{2,1,0:T(8,128)S(1)} %shard_map.37) | data formatting | bytes 147456

commit v14 on v13

--- a/solution.py
+++ b/solution.py
@@ -262,9 +262,16 @@
     for h in (1, 0):
         near_copy(h).start()
 
-    @pl.when(core == 0)
-    def _():
-        far_copy(0, 0).start()
+    def start_far(of_core_0, of_core_1):
+        @pl.when(core == 0)
+        def _():
+            far_copy(*of_core_0).start()
+
+        @pl.when(core == 1)
+        def _():
+            far_copy(*of_core_1).start()
+
+    start_far((0, 0), (1, 0))
 
     def lanes_of(h):
         return pl.ds(h * 256 if isinstance(h, int) else pl.multiple_of(h * 256, 256), 256)
@@ -283,11 +290,7 @@
         for h in range(2):
             near_copy(h).wait_recv()
 
-    @pl.when(core == 1)
-    def _():
-        far_copy(0, 0).start()
-
-    far_copy(0, 1).start()
+    start_far((0, 1), (0, 0))
 
     own_group = v // 8 == j
 
@@ -313,9 +316,10 @@
         lax.fori_loop(1, SHARDS, share_slab, 0)
         slab[v] = slab_sum[...]
 
-    far_copy(0, 2).start()
-    for q in range(QUADS):
-        far_copy(1, q).start()
+    start_far((0, 2), (0, 1))
+    start_far((1, 0), (0, 2))
+    far_copy(1, 1).start()
+    far_copy(1, 2).start()
 
     with jax.named_scope("places"):
         b = lax.broadcasted_iota(I32, (1, ROWS), 1)
@@ -474,13 +478,15 @@
             major, minor = offsets_at(step)
             return ahead_of(z, major) * 4 + ahead_of(x, minor)
 
-        def four(index, carry):
-            steps = [index * 4 + more for more in range(8)]
-            for step in steps[:4]:
+        size = 2 if n == 2 else 4
+
+        def some(index, carry):
+            steps = [index * size + more for more in range(2 * size)]
+            for step in steps[:size]:
                 block_of(n, id_at(step))
             if unfinished is not None:
-                standard(unfinished, [id_at(step & 15) for step in steps[4:]])
-            for step in steps[:4]:
+                standard(unfinished, [id_at(step & 15) for step in steps[size:]])
+            for step in steps[:size]:
                 major, minor = offsets_at(step)
                 m = ahead_of(z, major) * 4 + ahead_of(x, minor)
 
@@ -505,8 +511,8 @@
 
         with jax.named_scope("kernels"):
             if unfinished is not None:
-                standard(unfinished, [id_at(step) for step in range(4)])
-            lax.fori_loop(0, OWN // 4, four, 0)
+                standard(unfinished, [id_at(step) for step in range(size)])
+            lax.fori_loop(0, OWN // size, some, 0)
 
     def second_sums(n):
         z_rows, x_rows, y_rows = split[n]

time: 50 us -> 51 us (1.020)
  Pallas kernels: 49.2 us -> 50.2 us
    pallas_call x1, Pallas kernels: 49.2 us -> 50.2 us  [body(): pl.pallas_call(main_kernel, out_shape=pltpu.VMEM((2, EP * LOCAL, ROWS), F...]
where the time goes in v14:
time: 51 us; the launch traced here: 50.8 us
  Pallas kernels  50.2 us (98%)
  local copies, waits for them, and re-layouts  0.64 us (1%)
    pallas_call x1, Pallas kernels, body(): pl.pallas_call(main_kernel, out_shape=pltpu.VMEM((2, EP * LOCAL, ROWS), F...  50.2 us

profile of v14, /device:TPU:1, one launch (start us, length us, event | category | flops | bytes accessed | tf_op | source)
XLA Modules:
  0.0 50.8 jit_solution(9540067722332783552)
XLA Ops:
  0.0 50.2 %shard_map.37 = f32[2,48,192]{2,1,0:T(8,128)S(1)} custom-call(bf16[4,256,512]{2,1,0:T(8,128)(2,1)} %series_hbm.1, s32[16,12]{1,0:T(8,128)} %offsets_hbm.1, s32[64]{0:T(128)} %selected_hbm.1), custom_call_target="tpu_custom_call" | custom-call | tf_op jit(solution)/shard_map/pallas_call | solution.py:729
  50.2 0.6 %copy.5 = f32[2,48,192]{2,1,0:T(8,128)} copy(f32[2,48,192]{2,1,0:T(8,128)S(1)} %shard_map.37) | data formatting | bytes 147456

commit v15 on v10

--- a/solution.py
+++ b/solution.py
@@ -125,23 +125,16 @@
     turn_c,
     put_columns,
     load_sem,
-    slab_send,
+    sent,
     slab_recv,
-    share_send,
     share_recv,
-    near_send,
     near_recv,
-    far_send,
     far_recv,
-    relay_send,
     relay_recv,
-    part_send,
     z_recv,
     x_recv,
     y_recv,
-    sum_send,
     sum_recv,
-    final_send,
     final_recv,
 ):
     corr = (corr_even, corr_odd)
@@ -234,7 +227,7 @@
 
         @pl.when(jnp.logical_or(to_j != j, to_v != v))
         def _():
-            copy_to(slab_out.at[piece], slab_in.at[v], slab_send, slab_recv, to_j, to_v).start()
+            copy_to(slab_out.at[piece], slab_in.at[v], sent, slab_recv, to_j, to_v).start()
 
         return carry
 
@@ -242,17 +235,16 @@
         lax.fori_loop(0, SHARDS, send_slab, 0)
 
     def near_copy(h):
-        return copy_to(epochs.at[0, h], epochs.at[1, h], near_send.at[h], near_recv.at[h], near, v)
+        return copy_to(epochs.at[0, h], epochs.at[1, h], sent, near_recv, near, v)
 
     def far_copy(g, q):
         at = g * QUADS + q
         source, target = epochs.at[core ^ g, core, q], epochs.at[2 + g, core, q]
-        return copy_to(source, target, far_send.at[at], far_recv.at[at], far, v)
+        return copy_to(source, target, sent, far_recv.at[at], far, v)
 
     def relay_copy(g, q):
-        at = g * QUADS + q
         ref = epochs.at[2 + g, core, q]
-        return copy_to(ref, ref, relay_send.at[at], relay_recv.at[at], near, v)
+        return copy_to(ref, ref, sent, relay_recv.at[g], near, v)
 
     def relay(g, q):
         with jax.named_scope("relay"):
@@ -280,8 +272,7 @@
         scales(0, h)
 
     with jax.named_scope("near_wait"):
-        for h in range(2):
-            near_copy(h).wait_recv()
+        await_bytes(epochs.at[1], near_recv)
 
     @pl.when(core == 1)
     def _():
@@ -306,7 +297,7 @@
         slab_sum[...] = jnp.sum(slab_in[...].astype(F32), axis=0).astype(BF16)
 
     def share_slab(step, carry):
-        copy_to(slab_sum, slab.at[v], share_send, share_recv, j, (v + step) & (SHARDS - 1)).start()
+        copy_to(slab_sum, slab.at[v], sent, share_recv, j, (v + step) & (SHARDS - 1)).start()
         return carry
 
     with jax.named_scope("share_slab"):
@@ -488,18 +479,18 @@
                 def _():
                     source = gram[n].at[m, pl.ds(0, z_rows)]
                     to_v = shard_at(ahead_of(z, major), x, y)
-                    copy_to(source, z_parts[n].at[minor, major], part_send.at[n], z_recv.at[n, minor], j, to_v).start()
+                    copy_to(source, z_parts[n].at[minor, major], sent, z_recv.at[n * 4 + minor], j, to_v).start()
 
                 @pl.when(minor > 0)
                 def _():
                     source = gram[n].at[m, pl.ds(z_rows, x_rows)]
                     to_v = shard_at(z, ahead_of(x, minor), y)
-                    copy_to(source, x_parts[n].at[major, minor], part_send.at[n], x_recv.at[n, major], j, to_v).start()
+                    copy_to(source, x_parts[n].at[major, minor], sent, x_recv.at[n * 4 + major], j, to_v).start()
 
                 if y_rows:
                     rows = pl.ds(pl.multiple_of(z_rows + x_rows + y_rows // 2 * (y ^ 1), 8), y_rows // 2)
                     copy_to(
-                        gram[n].at[m, rows], y_parts.at[major * 4 + minor], part_send.at[n], y_recv.at[major], j, v ^ 1
+                        gram[n].at[m, rows], y_parts.at[major * 4 + minor], sent, y_recv.at[major], j, v ^ 1
                     ).start()
             return carry
 
@@ -514,7 +505,7 @@
         def along(step, block):
             parts, recv, sums = ((z_parts, z_recv, z_sums), (x_parts, x_recv, x_sums))[block]
             with jax.named_scope("part_wait"):
-                await_bytes(parts[n].at[step, pl.ds(1, 3)], recv.at[n, step])
+                await_bytes(parts[n].at[step, pl.ds(1, 3)], recv.at[n * 4 + step])
             own = (ahead_of(z, step) * 4 + x) if block else (z * 4 + ahead_of(x, step))
             own = gram[n][own, pl.ds(z_rows, x_rows) if block else pl.ds(0, z_rows), :]
             sums[n][step] = (own + parts[n][step, 1]) + (parts[n][step, 2] + parts[n][step, 3])
@@ -526,7 +517,7 @@
                 to_v = shard_at(ahead_of(z, step), x, side) if block else shard_at(z, ahead_of(x, step), side)
                 if slot:
                     copy_to(
-                        sums[n].at[step, rows], last[n][block].at[slot], sum_send.at[n], sum_recv.at[n, block], j, to_v
+                        sums[n].at[step, rows], last[n][block].at[slot], sent, sum_recv.at[n * 2 + block], j, to_v
                     ).start()
                 else:
                     last[n][block][0] = sums[n][0, rows, :]
@@ -542,7 +533,7 @@
                 if step:
                     y_sums[step] = added
                     copy_to(
-                        y_sums.at[step], y_last.at[step], sum_send.at[n], sum_recv.at[n, 2], j, shard_at(to_z, to_x, y)
+                        y_sums.at[step], y_last.at[step], sent, sum_recv.at[n * 2 + 2], j, shard_at(to_z, to_x, y)
                     ).start()
                 else:
                     y_last[0] = added
@@ -563,7 +554,7 @@
     def hand_over(n):
         with jax.named_scope("last_wait"):
             for block, ref in enumerate(last[n]):
-                await_bytes(ref.at[pl.ds(0, ref.shape[0] - 1)], sum_recv.at[n, block])
+                await_bytes(ref.at[pl.ds(0, ref.shape[0] - 1)], sum_recv.at[n * 2 + block])
         mean = 1.0 / (VOX * SHARDS)
         first = 0
         for ref in last[n]:
@@ -572,7 +563,7 @@
             first += rows
         for other in range(SUBJ):
             copy = copy_to(
-                total[n], final[n].at[place], final_send.at[n], final_recv.at[n], (j ^ other) if other else j, owner_v
+                total[n], final[n].at[place], sent, final_recv.at[n], (j ^ other) if other else j, owner_v
             )
             if other:
                 copy.start()
@@ -589,11 +580,11 @@
     def await_final(n, sem):
         @pl.when(owner_v == v)
         def _():
-            await_bytes(final[n].at[pl.ds(0, SUBJ - 1)], sem.at[n])
+            await_bytes(final[n].at[pl.ds(0, SUBJ - 1)], sem)
 
         @pl.when(owner_v != v)
         def _():
-            await_bytes(final[n], sem.at[n])
+            await_bytes(final[n], sem)
 
     def scores_of(correlated, finished):
         with jax.named_scope("scores"):
@@ -604,8 +595,7 @@
 
     def relayed(g):
         with jax.named_scope("relay_wait"):
-            for q in range(QUADS):
-                relay_copy(g, q).wait_recv()
+            await_bytes(epochs.at[2 + g, 1 - core], relay_recv.at[g])
 
     scores_of(0, None)
     scores_of(1, 0)
@@ -676,45 +666,40 @@
         return terms[0] + terms[1]
 
     with jax.named_scope("final"):
-        await_final(0, final_recv)
+        await_final(0, final_recv.at[0])
     with jax.named_scope("place"):
         for i in range(2):
             out_ref[i] = placed(0, i)
     hand_over(2)
     with jax.named_scope("final"):
-        await_final(1, final_recv)
+        await_final(1, final_recv.at[1])
     with jax.named_scope("place"):
         for i in range(2):
             out_ref[i] += placed(1, i)
     with jax.named_scope("final"):
-        await_final(2, final_recv)
+        await_final(2, final_recv.at[2])
     with jax.named_scope("place"):
         for i in range(2):
             out_ref[i] += placed(2, i)
 
     with jax.named_scope("drain"):
-        await_bytes(slab_in.at[pl.ds(0, SHARDS - 1)], share_send)
-
-        @pl.when(own_group)
-        def _():
-            await_bytes(slab_in.at[pl.ds(0, SHARDS - 1)], slab_send)
+        for ref in (slab_in.at[pl.ds(0, SHARDS - 1)], slab_in.at[pl.ds(0, SHARDS - 1)]):
+            await_bytes(ref, sent)
 
         @pl.when(jnp.logical_not(own_group))
         def _():
-            await_bytes(slab_in, slab_send)
-
+            await_bytes(slab_sum, sent)
+
+        for slot in range(2):
+            await_bytes(epochs.at[slot], sent)
+        await_bytes(epochs.at[2], sent)
         for n in range(3):
-            await_bytes(z_parts[n].at[pl.ds(0, 3)], part_send.at[n])
-            await_bytes(x_parts[n].at[pl.ds(0, 3)], part_send.at[n])
+            await_bytes(z_parts[n].at[pl.ds(0, 3)], sent)
+            await_bytes(x_parts[n].at[pl.ds(0, 3)], sent)
             for ref in last[n]:
-                await_bytes(ref.at[pl.ds(0, ref.shape[0] - 1)], sum_send.at[n])
-            await_final(n, final_send)
-        await_bytes(y_parts, part_send.at[2])
-        for h in range(2):
-            near_copy(h).wait_send()
-            for q in range(QUADS):
-                far_copy(h, q).wait_send()
-                relay_copy(h, q).wait_send()
+                await_bytes(ref.at[pl.ds(0, ref.shape[0] - 1)], sent)
+            await_final(n, sent)
+        await_bytes(y_parts, sent)
 
 
 def body(series, offsets, selected):
@@ -791,19 +776,12 @@
             dma,
             dma,
             dma,
+            dma((2 * QUADS,)),
             dma((2,)),
-            dma((2,)),
-            dma((2 * QUADS,)),
-            dma((2 * QUADS,)),
-            dma((2 * QUADS,)),
-            dma((2 * QUADS,)),
-            dma((3,)),
-            dma((3, 4)),
-            dma((3, 4)),
+            dma((12,)),
+            dma((12,)),
             dma((4,)),
-            dma((3,)),
-            dma((3, 3)),
-            dma((3,)),
+            dma((7,)),
             dma((3,)),
         ],
         compiler_params=pltpu.CompilerParams(collective_id=0, has_side_effects=True),

time: 49.9 us -> 49.6 us (level)
  no operation moved by 1% of the time
where the time goes in v15:
time: 49.6 us; the launch traced here: 49.5 us
  Pallas kernels  48.8 us (98%)
  local copies, waits for them, and re-layouts  0.64 us (1%)
    pallas_call x1, Pallas kernels, body(): pl.pallas_call(main_kernel, out_shape=pltpu.VMEM((2, EP * LOCAL, ROWS), F...  48.8 us

profile of v15, /device:TPU:1, one launch (start us, length us, event | category | flops | bytes accessed | tf_op | source)
XLA Modules:
  0.0 49.5 jit_solution(3098478366361953193)
XLA Ops:
  0.0 48.8 %shard_map.37 = f32[2,48,192]{2,1,0:T(8,128)S(1)} custom-call(bf16[4,256,512]{2,1,0:T(8,128)(2,1)} %series_hbm.1, s32[16,12]{1,0:T(8,128)} %offsets_hbm.1, s32[64]{0:T(128)} %selected_hbm.1), custom_call_target="tpu_custom_call" | custom-call | tf_op jit(solution)/shard_map/pallas_call | solution.py:708
  48.9 0.6 %copy.5 = f32[2,48,192]{2,1,0:T(8,128)} copy(f32[2,48,192]{2,1,0:T(8,128)S(1)} %shard_map.37) | data formatting | bytes 147456

commit v16 on v15

--- a/solution.py
+++ b/solution.py
@@ -479,13 +479,13 @@
                 def _():
                     source = gram[n].at[m, pl.ds(0, z_rows)]
                     to_v = shard_at(ahead_of(z, major), x, y)
-                    copy_to(source, z_parts[n].at[minor, major], sent, z_recv.at[n * 4 + minor], j, to_v).start()
+                    copy_to(source, z_parts[n].at[minor, major], sent, z_recv.at[minor + 2 if n == 2 else n], j, to_v).start()
 
                 @pl.when(minor > 0)
                 def _():
                     source = gram[n].at[m, pl.ds(z_rows, x_rows)]
                     to_v = shard_at(z, ahead_of(x, minor), y)
-                    copy_to(source, x_parts[n].at[major, minor], sent, x_recv.at[n * 4 + major], j, to_v).start()
+                    copy_to(source, x_parts[n].at[major, minor], sent, x_recv.at[major + 2 if n == 2 else n], j, to_v).start()
 
                 if y_rows:
                     rows = pl.ds(pl.multiple_of(z_rows + x_rows + y_rows // 2 * (y ^ 1), 8), y_rows // 2)
@@ -504,8 +504,9 @@
 
         def along(step, block):
             parts, recv, sums = ((z_parts, z_recv, z_sums), (x_parts, x_recv, x_sums))[block]
-            with jax.named_scope("part_wait"):
-                await_bytes(parts[n].at[step, pl.ds(1, 3)], recv.at[n * 4 + step])
+            if n == 2:
+                with jax.named_scope("part_wait"):
+                    await_bytes(parts[n].at[step, pl.ds(1, 3)], recv.at[step + 2])
             own = (ahead_of(z, step) * 4 + x) if block else (z * 4 + ahead_of(x, step))
             own = gram[n][own, pl.ds(z_rows, x_rows) if block else pl.ds(0, z_rows), :]
             sums[n][step] = (own + parts[n][step, 1]) + (parts[n][step, 2] + parts[n][step, 3])
@@ -543,8 +544,12 @@
                 along(major, 1)
                 from_side(major)
         else:
+            with jax.named_scope("part_wait"):
+                await_bytes(x_parts[n].at[pl.ds(0, 3)], x_recv.at[n])
             for step in (1, 3, 2, 0):
                 along(step, 1)
+            with jax.named_scope("part_wait"):
+                await_bytes(z_parts[n].at[pl.ds(0, 3)], z_recv.at[n])
         for step in (1, 3, 2, 0):
             along(step, 0)
 
@@ -778,8 +783,8 @@
             dma,
             dma((2 * QUADS,)),
             dma((2,)),
-            dma((12,)),
-            dma((12,)),
+            dma((6,)),
+            dma((6,)),
             dma((4,)),
             dma((7,)),
             dma((3,)),

time: 49.6 us -> 49.6 us (level)
  no operation moved by 1% of the time
where the time goes in v16:
time: 49.6 us; the launch traced here: 49.5 us
  Pallas kernels  48.8 us (98%)
  local copies, waits for them, and re-layouts  0.64 us (1%)
    pallas_call x1, Pallas kernels, body(): pl.pallas_call(main_kernel, out_shape=pltpu.VMEM((2, EP * LOCAL, ROWS), F...  48.8 us

profile of v16, /device:TPU:1, one launch (start us, length us, event | category | flops | bytes accessed | tf_op | source)
XLA Modules:
  0.0 49.5 jit_solution(2019483406587814469)
XLA Ops:
  0.0 48.8 %shard_map.37 = f32[2,48,192]{2,1,0:T(8,128)S(1)} custom-call(bf16[4,256,512]{2,1,0:T(8,128)(2,1)} %series_hbm.1, s32[16,12]{1,0:T(8,128)} %offsets_hbm.1, s32[64]{0:T(128)} %selected_hbm.1), custom_call_target="tpu_custom_call" | custom-call | tf_op jit(solution)/shard_map/pallas_call | solution.py:713
  48.8 0.6 %copy.5 = f32[2,48,192]{2,1,0:T(8,128)} copy(f32[2,48,192]{2,1,0:T(8,128)S(1)} %shard_map.37) | data formatting | bytes 147456

commit v17 on v16

--- a/solution.py
+++ b/solution.py
@@ -609,8 +609,8 @@
     relayed(0)
     scores_of(4, 3)
     relay(1, 0)
-    kernels(0)
-    scores_of(5, 4)
+    kernels(0, 4)
+    scores_of(5, None)
     kernels(1, 5)
     relay(1, 1)
     relay(1, 2)
@@ -624,6 +624,7 @@
     second_sums(2)
     hand_over(0)
     hand_over(1)
+    hand_over(2)
 
     straight = (((1,), (0,)), ((), ()))
     left = lax.broadcasted_iota(I32, (EP * LOCAL, 128), 1) < 64
@@ -675,7 +676,6 @@
     with jax.named_scope("place"):
         for i in range(2):
             out_ref[i] = placed(0, i)
-    hand_over(2)
     with jax.named_scope("final"):
         await_final(1, final_recv.at[1])
     with jax.named_scope("place"):

time: 49.6 us -> 49.6 us (level)
  no operation moved by 1% of the time
where the time goes in v17:
time: 49.6 us; the launch traced here: 49.5 us
  Pallas kernels  48.8 us (98%)
  local copies, waits for them, and re-layouts  0.64 us (1%)
    pallas_call x1, Pallas kernels, body(): pl.pallas_call(main_kernel, out_shape=pltpu.VMEM((2, EP * LOCAL, ROWS), F...  48.8 us

profile of v17, /device:TPU:1, one launch (start us, length us, event | category | flops | bytes accessed | tf_op | source)
XLA Modules:
  0.0 49.5 jit_solution(9082883402852514728)
XLA Ops:
  0.0 48.8 %shard_map.37 = f32[2,48,192]{2,1,0:T(8,128)S(1)} custom-call(bf16[4,256,512]{2,1,0:T(8,128)(2,1)} %series_hbm.1, s32[16,12]{1,0:T(8,128)} %offsets_hbm.1, s32[64]{0:T(128)} %selected_hbm.1), custom_call_target="tpu_custom_call" | custom-call | tf_op jit(solution)/shard_map/pallas_call | solution.py:713
  48.8 0.6 %copy.5 = f32[2,48,192]{2,1,0:T(8,128)} copy(f32[2,48,192]{2,1,0:T(8,128)S(1)} %shard_map.37) | data formatting | bytes 147456
